TPU v7x, 32 devices: a whole 2x2x4 slice. The times are simulated.
32 devices in a mesh: gx: 8 (over z, y), gy: 4 (over x, core).
Axes of the slice: x: 2, y: 2, z: 4, core: 2. Of those that a mesh axis runs over, the one named last changes fastest.
Arguments:
- basis: bfloat16 [40960, 120], P(('gx', 'gy')), may hold values from -0.03125 to 0.03125
- snapshots: bfloat16 [40960, 256], P(('gx', 'gy')), may hold values from -6 to 6
- derivatives: bfloat16 [40960, 256], P(('gx', 'gy')), may hold values from -24 to 24
- quad_pairs: int32 [2, 7260], replicated, may hold values from 0 to 119, as said below
- penalty: float32 [7381], replicated, may hold values from 0.5 to 8
Outputs:
- operator: float32 [120, 7381], replicated
Inputs may be any that keep to these rules, and one draw needn't show every extreme that they name: `quad_pairs`: every pair (i, j) with 0 <= i <= j < 120 stands in exactly one column, in an order drawn from the seed.
All inputs are finite; a program needn't handle non-finite values.
Results may differ from a plain program's by a relative error of at most 0.0003.
Values sent between devices are 32-bit elements; how exact they have to be, the bound alone decides.
No kernel may reach another device: no remote copies, remote signals or barrier semaphores. Data moves between devices by JAX's collectives and lax.ppermute only.
A program may use at most 64 MiB of HBM per device.

v0:
```python
import math

import jax
import jax.numpy as jnp
from jax import lax
from jax.sharding import PartitionSpec as P

ITERS = 2


highest = lax.Precision.HIGHEST


def feature_rows(index, coeffs, pairs):
    total = coeffs.shape[0]
    count = pairs.shape[1]
    linear = coeffs[jnp.clip(index - 1, 0, total - 1)]
    slot = jnp.clip(index - 1 - total, 0, count - 1)
    quad = coeffs[pairs[0, slot]] * coeffs[pairs[1, slot]]
    column = index[:, None]
    width = 1 + total + count
    return jnp.where(
        column == 0,
        jnp.float32(1.0),
        jnp.where(column <= total, linear, jnp.where(column < width, quad, jnp.float32(0.0))),
    )


def gram_block(rows, columns, coeffs, pairs, weights, blocks):
    snaps = coeffs.shape[1]
    left = feature_rows(rows, coeffs, pairs)
    grouped = columns.reshape(blocks, -1)
    row_weights = weights[rows][:, None]

    def one_block(cols):
        right = feature_rows(cols, coeffs, pairs)
        inner = (
            lax.dot_general(
                left,
                right,
                (((1,), (1,)), ((), ())),
                precision=highest,
                preferred_element_type=jnp.float32,
            )
            / snaps
        )
        return inner + jnp.where(rows[:, None] == cols[None, :], row_weights, jnp.float32(0.0))

    stacked = lax.map(one_block, grouped)
    return jnp.transpose(stacked, (1, 0, 2)).reshape(rows.shape[0], -1)


def column_sum(first, second):
    return jnp.sum(first * second, axis=0)


def on_device(basis, snapshots, derivatives, quad_pairs, penalty):
    across = lax.axis_size("gx")
    down = lax.axis_size("gy")
    devices = across * down
    order = basis.shape[1]
    snaps = snapshots.shape[1]
    width = 1 + order + quad_pairs.shape[1]
    piece = -(-width // devices)
    padded = piece * devices
    dims = (((0,), (0,)), ((), ()))
    coeff_part = lax.dot_general(basis, snapshots, dims, preferred_element_type=jnp.float32)
    rate_part = lax.dot_general(basis, derivatives, dims, preferred_element_type=jnp.float32)
    coeffs, rates = lax.psum((coeff_part, rate_part), ("gx", "gy"))
    weights = jnp.concatenate([penalty, jnp.ones((padded - width,), jnp.float32)])
    flat = lax.axis_index("gx") * down + lax.axis_index("gy")
    own = flat * piece + jnp.arange(piece, dtype=jnp.int32)
    own_rows = feature_rows(own, coeffs, quad_pairs)
    target = lax.dot_general(
        own_rows,
        rates,
        (((1,), (1,)), ((), ())),
        precision=highest,
        preferred_element_type=jnp.float32,
    ) / math.sqrt(snaps)
    block = padded // across
    rows = lax.axis_index("gx") * block + jnp.arange(block, dtype=jnp.int32)
    starts = jnp.arange(across, dtype=jnp.int32)[:, None] * down + lax.axis_index("gy")
    cols = (starts * piece + jnp.arange(piece, dtype=jnp.int32)[None, :]).reshape(-1)
    matrix = gram_block(rows, cols, coeffs, quad_pairs, weights, 1)

    def apply(vector):
        summed = jnp.dot(
            matrix,
            lax.all_gather(vector, "gx", axis=0, tiled=True),
            precision=highest,
            preferred_element_type=jnp.float32,
        )
        return lax.psum_scatter(summed, "gy", scatter_dimension=0, tiled=True)

    solution = jnp.zeros_like(target)
    residual = target

    def both_sums(vector, image):
        return lax.psum((column_sum(vector, vector), column_sum(vector, image)), ("gx", "gy"))

    image = apply(residual)
    norm_now, product = both_sums(residual, image)
    alpha = norm_now / product
    direction = residual
    along = image
    for step in range(ITERS):
        solution = solution + alpha * direction
        residual = residual - alpha * along
        if step + 1 < ITERS:
            image = apply(residual)
            norm_next, product = both_sums(residual, image)
            ratio = norm_next / norm_now
            alpha = norm_next / (product - ratio * norm_next / alpha)
            direction = residual + ratio * direction
            along = image + ratio * along
            norm_now = norm_next
    whole = lax.all_gather(solution, ("gx", "gy"), axis=0, tiled=True)
    return whole[:width].T


def solution(mesh):
    in_specs = (P(("gx", "gy"), None), P(("gx", "gy"), None), P(("gx", "gy"), None), P(), P())
    out_specs = P()
    return jax.shard_map(
        on_device, mesh=mesh, in_specs=in_specs, out_specs=out_specs, check_vma=False
    )
```

profile of v0, /device:TPU:0, one launch (start us, length us, event | category | flops | bytes accessed | tf_op | source)
XLA Modules:
  0.0 463.3 jit_solution(17693560194602072271)
XLA Ops:
  12.3 12.1 %gather_fusion.6 = s32[924]{0:T(1024)S(1)} fusion(s32[2,7260]{1,0:T(2,128)S(1)} %copy-done.2, s32[924]{0:T(1024)S(1)} %bitcast.34), kind=kCustom, calls=%fused_computation.6 | custom fusion | bytes 14784 | tf_op jit(solution)/shard_map/gather | solution.py:19
  24.4 12.1 %gather_fusion.8 = s32[924]{0:T(1024)S(1)} fusion(s32[2,7260]{1,0:T(2,128)S(1)} %copy-done.2, s32[924]{0:T(1024)S(1)} %bitcast.33), kind=kCustom, calls=%fused_computation.8 | custom fusion | bytes 14784 | tf_op jit(solution)/shard_map/gather | solution.py:19
  36.8 22.9 %gather_fusion.11 = s32[1848]{0:T(1024)S(1)} fusion(s32[2,7260]{1,0:T(2,128)S(1)} %copy-done.2, s32[1848]{0:T(1024)S(1)} %get-tuple-element.32), kind=kCustom, calls=%fused_computation.11 | custom fusion | bytes 29568 | tf_op jit(solution)/shard_map/while/body/eval_jaxpr/gather | solution.py:19
  59.8 22.9 %gather_fusion.13 = s32[1848]{0:T(1024)S(1)} fusion(s32[2,7260]{1,0:T(2,128)S(1)} %copy-done.2, s32[1848]{0:T(1024)S(1)} %get-tuple-element.23), kind=kCustom, calls=%fused_computation.13 | custom fusion | bytes 29568 | tf_op jit(solution)/shard_map/while/body/eval_jaxpr/gather | solution.py:19
  90.6 5.8 %gather_fusion.15 = f32[924]{0:T(1024)S(1)} fusion(f32[7392]{0:T(1024)S(1)} %concatenate.29, s32[1024]{0:T(1024)S(1)} %pad_clamp_fusion.3), kind=kCustom, calls=%fused_computation.15 | custom fusion | bytes 11088 | tf_op jit(solution)/shard_map/gather | solution.py:33
  96.5 45.0 %all-reduce.16.cloned.1.call-done = (f32[120,256]{1,0:T(8,128)}, f32[120,256]{1,0:T(8,128)}) async-done(((f32[120,256]{1,0:T(8,128)}, f32[120,256]{1,0:T(8,128)}), (f32[120,256]{1,0:T(8,128)}, f32[120,256]{1,0:T(8,128)})) %all-reduce.16.cloned.1.call-update) | async-done | bytes 245776 | tf_op jit(solution)/shard_map/psum | solution.py:69
  141.5 5.6 %gather_fusion.7 = f32[924,256]{1,0:T(8,128)} fusion(f32[120,256]{1,0:T(8,128)} %get-tuple-element.40, s32[1024]{0:T(1024)S(1)} %pad_clamp_fusion.5), kind=kCustom, calls=%fused_computation.7 | custom fusion | bytes 1896048 | tf_op jit(solution)/shard_map/gather | solution.py:19
  147.1 4.6 gather_fusion.9
  151.7 4.6 gather_fusion.5
  156.3 4.8 %gather_fusion.12 = f32[1848,256]{1,0:T(8,128)S(1)} fusion(f32[120,256]{1,0:T(8,128)S(1)} %copy-done.1, s32[2048]{0:T(1024)S(1)} %pad_clamp_fusion.1), kind=kCustom, calls=%fused_computation.12 | custom fusion | bytes 3792096 | tf_op jit(solution)/shard_map/while/body/eval_jaxpr/gather | solution.py:19
  161.1 5.8 %gather_fusion.14 = f32[1848,256]{1,0:T(8,128)} fusion(f32[120,256]{1,0:T(8,128)S(1)} %copy-done.1, s32[2048]{0:T(1024)S(1)} %pad_clamp_fusion), kind=kCustom, calls=%fused_computation.14 | custom fusion | bytes 3792096 | tf_op jit(solution)/shard_map/while/body/eval_jaxpr/gather | solution.py:19
  166.9 5.7 %gather_fusion.10 = f32[1848,256]{1,0:T(8,128)} fusion(f32[120,256]{1,0:T(8,128)S(1)} %copy-done.1, s32[2048]{0:T(1024)S(1)} %pad_clamp_fusion.2), kind=kCustom, calls=%fused_computation.10 | custom fusion | bytes 3792096 | tf_op jit(solution)/shard_map/while/body/eval_jaxpr/gather | solution.py:17
  177.2 33.0 %all-gather = f32[8,231,120]{2,1,0:T(8,128)S(1)} all-gather(f32[1,231,120]{2,1,0:T(8,128)S(1)} %multiply_bitcast_fusion), channel_id=1, replica_groups=mesh['gx'=8,'gy'=4] {'gx'}, dimensions={0}, use_global_device_ids=true | all-gather | bytes 997920 | tf_op jit(solution)/shard_map/all_gather | solution.py:90
  211.2 10.2 %fusion.14 = f32[924,1848]{1,0:T(8,128)S(1)} fusion(f32[1848,256]{1,0:T(8,128)} %gather_fusion.10, f32[1848,256]{1,0:T(8,128)S(1)} %gather_fusion.12, f32[1848,256]{1,0:T(8,128)} %gather_fusion.14, f32[924,256]{1,0:T(8,128)} %gather_fusion.5, f32[924,256]{1,0:T(8,128)} %gather_fusion.7, f32[924,256]{1,0:T(8,128)} %gather_fusion.9, ...), kind=kOutput, calls=%fused_computation.29 | convolution fusion | flops 5248438272 | bytes 15354108 | tf_op jit(solution)/shard_map/while/body/eval_jaxpr/dot_general | solution.py:38
  224.3 6.8 %fusion.3 = f32[924,120]{1,0:T(8,128)S(1)} fusion(f32[1848,120]{1,0:T(8,128)S(1)} %copy-done.6, f32[924,1848]{1,0:T(8,128)S(1)} %fusion.14, f32[924]{0:T(1024)S(1)} %gather_fusion.15, s32[1848]{0:T(1024)S(1)} %add.389, s32[924]{0:T(1024)S(1)} %iota_add_fusion.2), kind=kOutput, calls=%fused_computation.18 | convolution fusion | flops 2465704960 | bytes 8175552 | tf_op jit(solution)/shard_map/dot_general | solution.py:88
  231.2 10.8 %fusion = f32[240,120]{1,0:T(8,128)S(1)} fusion(f32[924,120]{1,0:T(8,128)S(1)} %fusion.3), kind=kCustom, calls=%all-reduce-scatter | all-reduce-scatter fusion | flops 115201 | bytes 559232
  245.0 40.9 %all-reduce.12 = (f32[120]{0:T(128)S(1)}, f32[120]{0:T(128)S(1)}) all-reduce(f32[120]{0:T(128)S(1)} %get-tuple-element.22, f32[120]{0:T(128)S(1)} %get-tuple-element.21), channel_id=1, replica_groups=mesh['gx'=8,'gy'=4] {'gx','gy'}, use_global_device_ids=true, to_apply=%region_3.4 | all-reduce | flops 240 | bytes 1920 | tf_op jit(solution)/shard_map/psum | solution.py:100
  285.9 32.5 %all-gather.1 = f32[8,231,120]{2,1,0:T(8,128)S(1)} all-gather(f32[1,231,120]{2,1,0:T(8,128)S(1)} %bitcast.37), channel_id=1, replica_groups=mesh['gx'=8,'gy'=4] {'gx'}, dimensions={0}, use_global_device_ids=true | all-gather | bytes 997920 | tf_op jit(solution)/shard_map/all_gather | solution.py:90
  318.4 8.9 %fusion.2 = f32[924,120]{1,0:T(8,128)S(1)} fusion(f32[1848,120]{1,0:T(8,128)S(1)} %reshape.440, f32[924,1848]{1,0:T(8,128)} %copy-done.3, f32[924]{0:T(1024)S(1)} %gather_fusion.15, s32[1848]{0:T(1024)S(1)} %add.389, s32[924]{0:T(1024)S(1)} %iota_add_fusion.2), kind=kOutput, calls=%fused_computation.17 | convolution fusion | flops 2465704960 | bytes 8175552 | tf_op jit(solution)/shard_map/dot_general | solution.py:88
  327.4 11.0 %fusion.1 = f32[240,120]{1,0:T(8,128)S(1)} fusion(f32[924,120]{1,0:T(8,128)S(1)} %fusion.2), kind=kCustom, calls=%all-reduce-scatter.1 | all-reduce-scatter fusion | flops 115201 | bytes 559232
  340.9 40.6 %all-reduce.11 = (f32[120]{0:T(128)S(1)}, f32[120]{0:T(128)S(1)}) all-reduce(f32[120]{0:T(128)S(1)} %get-tuple-element.20, f32[120]{0:T(128)S(1)} %get-tuple-element.19), channel_id=1, replica_groups=mesh['gx'=8,'gy'=4] {'gx','gy'}, use_global_device_ids=true, to_apply=%region_8.9 | all-reduce | flops 240 | bytes 1920 | tf_op jit(solution)/shard_map/psum | solution.py:100
  382.2 61.4 %all-gather.5.cloned.1.call-done = f32[32,231,120]{2,1,0:T(8,128)} async-done(((f32[1,231,120]{2,1,0:T(8,128)}), f32[32,231,120]{2,1,0:T(8,128)}) %all-gather.5.cloned.1.call-update) | async-done | bytes 3548176 | tf_op jit(solution)/shard_map/all_gather | solution.py:118
  447.1 4.1 slice.36
  451.3 5.2 %copy.10 = f32[7381,120]{0,1:T(8,128)} copy(f32[7381,120]{1,0:T(8,128)} %slice.36) | data formatting | bytes 7085760
  (86 shorter events, 31.4 us)
Async XLA Ops:
  6.5 1.1 copy-start
  6.5 5.8 %copy-start.2 = (s32[2,7260]{1,0:T(2,128)S(1)}, s32[2,7260]{1,0:T(2,128)}, u32[]{:S(2)}) copy-start(s32[2,7260]{1,0:T(2,128)} %param.8) | copy-start | bytes 174244
  6.5 135.0 %all-reduce.16.cloned.1.call-start = ((), (), s32[]{:S(2)}) async-start(), calls=%async_computation.1 | async-start | bytes 491520 | tf_op jit(solution)/shard_map/psum | solution.py:69
  11.6 432.0 %all-gather.5.cloned.1.call-start = ((), (), s32[]{:S(2)}) async-start(), calls=%async_computation | async-start | bytes 3919872 | tf_op jit(solution)/shard_map/all_gather | solution.py:118
  59.8 30.8 %copy-start.8 = (f32[7381]{0:T(1024)S(1)}, f32[7381]{0:T(1024)}, u32[]{:S(2)}) copy-start(f32[7381]{0:T(1024)} %param.9) | copy-start | bytes 88576
  141.5 5.6 %copy-start.1 = (f32[120,256]{1,0:T(8,128)S(1)}, f32[120,256]{1,0:T(8,128)}, u32[]{:S(2)}) copy-start(f32[120,256]{1,0:T(8,128)} %get-tuple-element.40) | copy-start | bytes 368644
  172.6 2.8 copy-start.7
  176.5 0.7 copy-start.4
  211.2 13.1 %copy-start.6 = (f32[1848,120]{1,0:T(8,128)S(1)}, f32[1848,120]{1,0:T(8,128)}, u32[]{:S(2)}) copy-start(f32[1848,120]{1,0:T(8,128)} %reshape.438) | copy-start | bytes 2661124
  221.4 2.9 copy-start.3
  224.3 18.9 %copy-start.9 = (u32[32]{0:T(128)S(1)}, u32[32]{0:T(128)}, u32[]{:S(2)}) copy-start(u32[32]{0:T(128)} %constant.203) | copy-start | bytes 388
  224.3 20.6 %copy-start.5 = (f32[231,120]{1,0:T(8,128)S(1)}, f32[231,120]{1,0:T(8,128)}, u32[]{:S(2)}) copy-start(f32[231,120]{1,0:T(8,128)} %copy-done.4) | copy-start | bytes 332644
  242.0 2.5 collective-permute-start
  338.4 2.1 collective-permute-start.1
Sparse Core Ops, SparseCore 0:
  12.9 128.5 all-reduce.15
  382.3 61.2 all-gather.4
where the time goes:
time: 464 us; the launch traced here: 463 us
  blocking collectives  169 us (36%)
  local copies, waits for them, and re-layouts  137 us (30%)
  waiting for transfers between devices  107 us (23%)
  matrix products  31 us (7%)
  between operations  14.5 us (3%)
    gather x12, local copies, waits for them, and re-layouts, feature_rows(): quad = coeffs[pairs[0, slot]] * coeffs[pairs[1, slot]]  99.6 us
    psum x2, blocking collectives, both_sums(): lax.psum((column_sum(vector, vector), column_sum(vector, image)), ('gx',...  81.4 us
    all_gather x2, blocking collectives, apply(): lax.all_gather(vector, 'gx', axis=0, tiled=True)  65.5 us
    all_gather x1, waiting for transfers between devices, on_device(): whole = lax.all_gather(solution, ('gx', 'gy'), axis=0, tiled=True)  61.4 us
    psum x1, waiting for transfers between devices, on_device(): coeffs, rates = lax.psum((coeff_part, rate_part), ('gx', 'gy'))  45 us
    unnamed x2, blocking collectives  21.7 us
    unnamed x29, local copies, waits for them, and re-layouts  15.9 us
    dot_general x2, matrix products, apply(): jnp.dot(matrix, lax.all_gather(vector, 'gx', axis=0, tiled=True), precisi...  15.8 us
  transfers between devices with their start and end apart: 4, of which 3 were waited for; matrix products, arithmetic and copies ran while one was open for 18% of the time, Pallas kernels for 0%

commit v1 on v0

v1 whole, which is shorter than its diff:
```python
import math

import jax
import jax.numpy as jnp
from jax import lax
from jax.experimental import pallas as pl
from jax.experimental.pallas import tpu as pltpu
from jax.sharding import PartitionSpec as P

LANES = 128
TILE = 256
HIGHEST = lax.Precision.HIGHEST
F32 = jnp.float32
BF16 = jnp.bfloat16


def round_up(value, unit):
    return -(-value // unit) * unit


def dot(a, b, contract, precision=None):
    return lax.dot_general(
        a, b, (contract, ((), ())), precision=precision, preferred_element_type=F32
    )


def split(value):
    high = value.astype(BF16)
    return high, (value - high.astype(F32)).astype(BF16)


def project(basis_ref, snaps_ref, rates_ref, out_ref):
    order = basis_ref.shape[1]
    basis = basis_ref[...]
    out_ref[...] = jnp.zeros_like(out_ref)
    out_ref[0, :order, :] = dot(basis, snaps_ref[...], ((0,), (0,)))
    out_ref[1, :order, :] = dot(basis, rates_ref[...], ((0,), (0,)))


def pick(table, index):
    return jnp.take_along_axis(table, index, axis=1, mode="promise_in_bounds")


def fit(order, width, sums_ref, index_ref, weight_ref, out_ref, table_ref, left_ref, b_ref, s_ref, v_ref, acc_ref):
    snaps = sums_ref.shape[2]
    padded = index_ref.shape[1]
    tiles = padded // TILE
    lane = lax.broadcasted_iota(jnp.int32, (snaps, LANES), 1)
    linear = jnp.where(lane < order, jnp.transpose(sums_ref[0]), 0.0)
    table_ref[...] = jnp.where(lane == order, 1.0, linear)
    cross = dot(linear, linear, ((1,), (1,)), HIGHEST)
    squares = linear * linear
    gram = 1.0 + cross + 0.5 * (cross * cross + dot(squares, squares, ((1,), (1,)), HIGHEST))
    rates = sums_ref[1, :order, :] * (1.0 / math.sqrt(snaps))
    u = dot(rates, gram, ((1,), (0,)), HIGHEST)
    m0 = jnp.sum(rates * u, axis=1, keepdims=True)
    shift = jnp.sum(u * u, axis=1, keepdims=True) / (snaps * m0)
    along = u * (1.0 / snaps) - shift * rates
    mean = jnp.sum(weight_ref[...], axis=1, keepdims=True) * (1.0 / width)
    high, low = split(rates)
    left_ref[0:order, :] = high
    left_ref[2 * order : 3 * order, :] = low
    high, low = split(along)
    left_ref[order : 2 * order, :] = high
    left_ref[3 * order : 4 * order, :] = low
    v_ref[...] = jnp.zeros_like(v_ref)
    acc_ref[...] = jnp.zeros_like(acc_ref)

    def tile(step, carry):
        base = pl.multiple_of(step * TILE, TILE)
        table = table_ref[...]
        parts = []
        for half in range(TILE // LANES):
            place = pl.ds(pl.multiple_of(base + half * LANES, LANES), LANES)
            first = jnp.broadcast_to(index_ref[0:1, place], table.shape)
            second = jnp.broadcast_to(index_ref[1:2, place], table.shape)
            parts.append(pick(table, first) * pick(table, second))
        data = jnp.concatenate(parts, axis=1)
        data_high, data_low = split(data)
        one = dot(left_ref[...], data_high, ((1,), (0,)))
        two = dot(left_ref[0 : 2 * order, :], data_low, ((1,), (0,)))
        both = one[: 2 * order] + one[2 * order :] + two
        place = pl.ds(base, TILE)
        b = both[:order]
        extra = weight_ref[0:1, place] - mean
        scaled = extra * b
        s = both[order:] + scaled
        b_ref[:, place] = b
        s_ref[:, place] = s
        v_ref[...] += dot(scaled.astype(BF16), data_high, ((1,), (1,)))
        acc_ref[0] += scaled * b
        acc_ref[1] += s * s
        acc_ref[2] += extra * s * s
        acc_ref[3] += scaled * s
        return carry

    lax.fori_loop(0, tiles, tile, 0)
    total = [jnp.sum(acc_ref[k], axis=1, keepdims=True) for k in range(4)]
    bb_extra, ss, ss_extra, bs_extra = total
    ratio = bb_extra / m0
    alpha0 = 1.0 / (shift + mean + ratio)
    perp = ss - ratio * bb_extra
    image = dot(along, gram, ((1,), (0,)), HIGHEST) + v_ref[...] - ratio * u
    energy = (
        jnp.sum(image * image, axis=1, keepdims=True) * (1.0 / snaps)
        + mean * perp
        + ss_extra
        - 2.0 * ratio * bs_extra
        + ratio * ratio * bb_extra
    )
    rr1 = alpha0 * alpha0 * perp
    beta = rr1 / m0
    alpha1 = rr1 / (alpha0 * alpha0 * energy - rr1 * beta / alpha0)
    on_b = alpha0 + alpha1 * (beta + alpha0 * ratio)
    on_s = -alpha1 * alpha0

    def combine(step, carry):
        place = pl.ds(pl.multiple_of(step * TILE, TILE), TILE)
        out_ref[:, place] = on_b * b_ref[:, place] + on_s * s_ref[:, place]
        return carry

    whole = width // TILE
    lax.fori_loop(0, whole, combine, 0)
    if whole * TILE < width:
        rest = slice(whole * TILE, width)
        out_ref[:, rest] = on_b * b_ref[:, rest] + on_s * s_ref[:, rest]


def on_device(basis, snapshots, derivatives, quad_pairs, penalty):
    axes = ("gx", "gy")
    devices = lax.axis_size("gx") * lax.axis_size("gy")
    order = basis.shape[1]
    snaps = snapshots.shape[1]
    count = quad_pairs.shape[1]
    width = 1 + order + count
    padded = round_up(width, TILE)
    assert order + 2 <= LANES
    part = pl.pallas_call(
        project,
        out_shape=jax.ShapeDtypeStruct((2, LANES, snaps), F32),
        name="project",
    )(basis, snapshots, derivatives)
    rows = 2 * LANES
    full = round_up(rows, devices)
    pieces = jnp.pad(part.reshape(rows, snaps), ((0, full - rows), (0, 0)))
    pieces = pieces.reshape(devices, full // devices, snaps)
    pieces = lax.all_to_all(pieces, axes, 0, 0, tiled=True)
    summed = jnp.sum(pieces, axis=0, keepdims=True)
    spread = jnp.broadcast_to(summed, pieces.shape)
    whole = lax.all_to_all(spread, axes, 0, 0, tiled=True)
    sums = whole.reshape(full, snaps)[:rows].reshape(2, LANES, snaps)
    counting = jnp.arange(order, dtype=jnp.int32)
    ones = jnp.full((1 + order,), order, jnp.int32)
    blank = jnp.full((2, padded - width), order + 1, jnp.int32)
    head = jnp.stack([jnp.concatenate([ones[:1], counting]), ones])
    index = jnp.concatenate([head, quad_pairs, blank], axis=1)
    weight = jnp.pad(penalty, (0, padded - width)).reshape(1, padded)
    return pl.pallas_call(
        lambda *refs: fit(order, width, *refs),
        out_shape=jax.ShapeDtypeStruct((order, width), F32),
        scratch_shapes=[
            pltpu.VMEM((snaps, LANES), F32),
            pltpu.VMEM((4 * order, snaps), BF16),
            pltpu.VMEM((order, padded), F32),
            pltpu.VMEM((order, padded), F32),
            pltpu.VMEM((order, snaps), F32),
            pltpu.VMEM((4, order, TILE), F32),
        ],
        compiler_params=pltpu.CompilerParams(vmem_limit_bytes=48 * 2**20),
        name="fit",
    )(sums, index, weight)


def solution(mesh):
    split_rows = P(("gx", "gy"), None)
    return jax.shard_map(
        on_device,
        mesh=mesh,
        in_specs=(split_rows, split_rows, split_rows, P(), P()),
        out_specs=P(),
        check_vma=False,
    )
```

time: 464 us -> 61.4 us (0.13)
  blocking collectives: 169 us -> 17.9 us
  local copies, waits for them, and re-layouts: 137 us -> 2.82 us
  waiting for transfers between devices: 107 us -> 10.3 us
  matrix products: 31 us -> 0 us
  Pallas kernels: 0 us -> 27.4 us
  between operations: 14.5 us -> 0.07 us
    gather x16 -> x0, local copies, waits for them, and re-layouts: 117 us -> none  [the longest x12 99.6 us: feature_rows(): quad = coeffs[pairs[0, slot]] * coeffs[pairs[1, slot]]]
    psum x2 -> x0, blocking collectives: 81.4 us -> none  [both_sums(): lax.psum((column_sum(vector, vector), column_sum(vector, image)), ('gx',...]
    all_gather x2 -> x0, blocking collectives: 65.5 us -> none  [apply(): lax.all_gather(vector, 'gx', axis=0, tiled=True)]
    all_gather x1 -> x0, waiting for transfers between devices: 61.4 us -> none  [on_device(): whole = lax.all_gather(solution, ('gx', 'gy'), axis=0, tiled=True)]
    psum x1 -> x0, waiting for transfers between devices: 45 us -> none  [on_device(): coeffs, rates = lax.psum((coeff_part, rate_part), ('gx', 'gy'))]
    dot_general x6 -> x0, matrix products: 31 us -> none  [the longest x2 15.8 us: apply(): jnp.dot(matrix, lax.all_gather(vector, 'gx', axis=0, tiled=True), precisi...]
    pallas_call x0 -> x2, Pallas kernels: none -> 27.4 us  [the longest x1 24.9 us: on_device(): pl.pallas_call(lambda *refs: fit(order, width, *refs), out_shape=jax.Shap...]
    unnamed x2 -> x0, blocking collectives: 21.7 us -> none
  transfers between devices with their start and end apart: 4 -> 1, of which waited for: 3 -> 1; matrix products, arithmetic and copies ran while one was open for 18% -> 0% of each run, Pallas kernels for 0% -> 0%
where the time goes in v1:
time: 61.4 us; the launch traced here: 61.1 us
  Pallas kernels  27.4 us (45%)
  blocking collectives  17.9 us (29%)
  waiting for transfers between devices  10.3 us (17%)
  local copies, waits for them, and re-layouts  2.82 us (5%)
  starting transfers between devices  2.59 us (4%)
    pallas_call x1, Pallas kernels, on_device(): pl.pallas_call(lambda *refs: fit(order, width, *refs), out_shape=jax.Shap...  24.9 us
    all_to_all x1, blocking collectives, on_device(): pieces = lax.all_to_all(pieces, axes, 0, 0, tiled=True)  17.9 us
    all_to_all x1, waiting for transfers between devices, on_device(): whole = lax.all_to_all(spread, axes, 0, 0, tiled=True)  10.3 us
    all_to_all x1, starting transfers between devices, on_device(): whole = lax.all_to_all(spread, axes, 0, 0, tiled=True)  2.59 us
    pallas_call x1, Pallas kernels, on_device(): pl.pallas_call(project, out_shape=jax.ShapeDtypeStruct((2, LANES, snaps),...  2.43 us
    unnamed x7, local copies, waits for them, and re-layouts  1.9 us
  transfers between devices with their start and end apart: 1, of which 1 were waited for; matrix products, arithmetic and copies ran while one was open for 0% of the time, Pallas kernels for 0%

profile of v1, /device:TPU:0, one launch (start us, length us, event | category | flops | bytes accessed | tf_op | source)
XLA Modules:
  0.0 61.1 jit_solution(15407155823470614544)
XLA Ops:
  0.0 0.0 copy-start.2
  0.0 0.0 copy-start.1
  0.0 0.0 copy-start
  0.0 1.9 %copy.6.basis_ref = bf16[1280,120]{1,0:T(8,128)(2,1)} copy(bf16[1280,120]{0,1:T(8,128)(2,1)} %param.5) | data formatting | bytes 614400 | tf_op args[0]
  1.9 2.4 %project.1 = f32[2,128,256]{2,1,0:T(8,128)} custom-call(bf16[1280,120]{1,0:T(8,128)(2,1)} %copy.6.basis_ref, bf16[1280,256]{1,0:T(8,128)(2,1)} %snaps_ref.1, bf16[1280,256]{1,0:T(8,128)(2,1)} %rates_ref.1), custom_call_target="tpu_custom_call" | custom-call | tf_op jit(solution)/shard_map/project/pallas_call | solution.py:138
  4.3 17.9 %all_to_all.10 = f32[32,8,256]{2,1,0:T(8,128)S(1)} all-to-all(f32[32,8,256]{2,1,0:T(8,128)} %bitcast.3), channel_id=1, replica_groups=mesh['gx'=8,'gy'=4] {'gx','gy'}, dimensions={0} | all-to-all | bytes 524288 | tf_op jit(solution)/shard_map/all_to_all | solution.py:147
  22.3 0.7 %broadcast_in_dim.4 = f32[32,8,256]{2,1,0:T(8,128)} broadcast(f32[8,256]{1,0:T(8,128)S(1)} %reduce_sum.9), dimensions={1,2} | broadcast | bytes 270336 | tf_op jit(solution)/shard_map/broadcast_in_dim | solution.py:149
  23.0 2.6 %all-to-all-start.1 = ((f32[32,8,256]{2,1,0:T(8,128)}), f32[32,8,256]{2,1,0:T(8,128)S(1)}, u32[]{:S(2)}, u32[]{:S(2)}) async-start(f32[32,8,256]{2,1,0:T(8,128)} %broadcast_in_dim.4), calls=%async_computation.1 | async-start | bytes 524288 | tf_op jit(solution)/shard_map/all_to_all | solution.py:150
  25.6 0.0 copy-done.1
  25.7 0.0 copy-done.2
  25.7 0.0 copy-done
  25.7 0.2 concatenate.4.refs_1_
  25.9 10.3 %all-to-all-done.1 = f32[32,8,256]{2,1,0:T(8,128)S(1)} async-done(((f32[32,8,256]{2,1,0:T(8,128)}), f32[32,8,256]{2,1,0:T(8,128)S(1)}, u32[]{:S(2)}, u32[]{:S(2)}) %all-to-all-start.1) | async-done | bytes 262176 | tf_op jit(solution)/shard_map/all_to_all | solution.py:150
  36.2 24.9 %fit.1 = f32[120,7381]{1,0:T(8,128)} custom-call(f32[2,128,256]{2,1,0:T(8,128)S(1)} %bitcast.2, s32[2,7424]{1,0:T(2,128)S(1)} %concatenate.4.refs_1_, f32[1,7424]{1,0:T(1,128)S(1)} %reshape.10.refs_2_), custom_call_target="tpu_custom_call" | custom-call | tf_op jit(solution)/shard_map/fit/pallas_call | solution.py:158
  (4 shorter events, 0.1 us)
Async XLA Ops:
  0.0 25.7 %copy-start.2 = (s32[2,121]{1,0:T(2,128)S(1)}, s32[2,121]{1,0:T(2,128)}, u32[]{:S(2)}) copy-start(s32[2,121]{1,0:T(2,128)} %constant.10.clone.1) | copy-start | bytes 2908
  0.0 25.6 %copy-start.1 = (f32[7381]{0:T(1024)S(1)}, f32[7381]{0:T(1024)}, u32[]{:S(2)}) copy-start(f32[7381]{0:T(1024)} %param.9) | copy-start | bytes 88576
  0.0 25.7 %copy-start = (s32[2,7260]{1,0:T(2,128)S(1)}, s32[2,7260]{1,0:T(2,128)}, u32[]{:S(2)}) copy-start(s32[2,7260]{1,0:T(2,128)} %param.8) | copy-start | bytes 174244
  23.0 13.2 %all-to-all-start.1 = ((f32[32,8,256]{2,1,0:T(8,128)}), f32[32,8,256]{2,1,0:T(8,128)S(1)}, u32[]{:S(2)}, u32[]{:S(2)}) async-start(f32[32,8,256]{2,1,0:T(8,128)} %broadcast_in_dim.4), calls=%async_computation.1 | async-start | bytes 524288 | tf_op jit(solution)/shard_map/all_to_all | solution.py:150

commit v2 on v1

v2 whole, which is shorter than its diff:
```python
import math

import jax
import jax.numpy as jnp
from jax import lax
from jax.experimental import pallas as pl
from jax.experimental.pallas import tpu as pltpu
from jax.sharding import PartitionSpec as P

LANES = 128
TILE = 256
F32 = jnp.float32
BF16 = jnp.bfloat16
ROWS = ((1,), (0,))


def limit(mebibytes):
    return pltpu.CompilerParams(vmem_limit_bytes=mebibytes * 2**20)


def round_up(value, unit):
    return -(-value // unit) * unit


def dot(a, b, contract=ROWS):
    return lax.dot_general(a, b, (contract, ((), ())), preferred_element_type=F32)


def split(value):
    high = value.astype(BF16)
    return high, (value - high.astype(F32)).astype(BF16)


def project(basis_ref, snaps_ref, rates_ref, out_ref, basis_buf, snaps_buf, rates_buf, sems):
    order = basis_ref.shape[0]
    count, size = sems.shape[0], snaps_buf.shape[0] // sems.shape[0]
    copies = []
    for k in range(count):
        here = pl.ds(k * size, size)
        mine = [
            pltpu.make_async_copy(basis_ref.at[:, here], basis_buf.at[:, here], sems.at[k, 0]),
            pltpu.make_async_copy(snaps_ref.at[here, :], snaps_buf.at[here, :], sems.at[k, 1]),
            pltpu.make_async_copy(rates_ref.at[here, :], rates_buf.at[here, :], sems.at[k, 2]),
        ]
        for copy in mine:
            copy.start()
        copies.append(mine)
    total = [0.0, 0.0]
    for k in range(count):
        for copy in copies[k]:
            copy.wait()
        here = slice(k * size, (k + 1) * size)
        basis = basis_buf[:, here]
        total = [t + dot(basis, buf[here, :]) for t, buf in zip(total, (snaps_buf, rates_buf))]
    for k in range(2):
        out_ref[k, :order, :] = total[k]
        out_ref[k, order:, :] = jnp.zeros((LANES - order, out_ref.shape[2]), F32)


def add_up(parts_ref, out_ref):
    out_ref[...] = jnp.broadcast_to(jnp.sum(parts_ref[...], axis=0, keepdims=True), out_ref.shape)


def fit(
    sums_ref, index_ref, weight_ref, out_ref,
    table_ref, left_ref, gram_ref, high_ref, low_ref, b_ref, s_ref, v_ref, acc_ref, extra_ref, mix_ref, x_ref, sems,
):
    order, width = out_ref.shape
    snaps = sums_ref.shape[2]
    padded = index_ref.shape[1]
    pairs = padded // (2 * TILE)
    spare = padded // TILE - 2 * pairs

    def place(start, size):
        return pl.ds(start if isinstance(start, int) else pl.multiple_of(start, TILE), size)

    def build(start):
        here = place(start, TILE)
        row = lax.broadcasted_iota(jnp.int32, (LANES, TILE), 0)
        factors = []
        for k in range(2):
            hot = jnp.where(row == index_ref[k : k + 1, here], 1.0, 0.0).astype(BF16)
            factors.append(dot(table_ref[...], jnp.concatenate([hot, hot], axis=0)))
        high, low = split(factors[0] * factors[1])
        high_ref[:, here] = high
        low_ref[:, here] = low

    def multiply(start):
        here = place(start, TILE)
        one = dot(left_ref[...], high_ref[:, here])
        two = dot(left_ref[0 : 2 * order, :], low_ref[:, here])
        both = one[: 2 * order] + one[2 * order :] + two
        b = both[:order]
        b_ref[:, here] = b
        s_ref[:, here] = both[order:] + extra_ref[0:1, here] * b

    def gather(start, size):
        here = place(start, size)
        b = b_ref[:, here]
        s = s_ref[:, here]
        extra = extra_ref[0:1, here]
        scaled = extra * b
        v_ref[...] += dot(scaled.astype(BF16), high_ref[:, here], ((1,), (1,)))
        square = s * s
        for k, term in enumerate((scaled * b, square, extra * square, scaled * s)):
            acc_ref[k] += sum(term[:, i : i + LANES] for i in range(0, size, LANES))

    def on_pair(stage, index):
        for half in range(2):
            stage((2 * index + half) * TILE)

    coeffs = sums_ref[0]
    coeffs_high, coeffs_low = split(coeffs)
    high, low = split(jnp.transpose(coeffs))
    lane = lax.broadcasted_iota(jnp.int32, (snaps, LANES), 1)
    table_ref[:, :LANES] = jnp.where(lane == order, 1.0, high.astype(F32)).astype(BF16)
    table_ref[:, LANES:] = low
    mean = jnp.sum(weight_ref[...], axis=1, keepdims=True) * (1.0 / width)
    extra_ref[...] = weight_ref[...] - mean
    v_ref[...] = jnp.zeros_like(v_ref)
    acc_ref[...] = jnp.zeros_like(acc_ref)
    on_pair(build, 0)
    on_pair(build, 1)
    if spare:
        build(2 * pairs * TILE)
    table = table_ref[...]
    cross = dot(table, jnp.concatenate([coeffs_high, coeffs_high], axis=0)) + dot(high, coeffs_low)
    square = coeffs * coeffs
    square_high, square_low = split(square)
    turned_high, turned_low = split(jnp.transpose(square))
    squares = dot(
        jnp.concatenate([turned_high, turned_low], axis=1),
        jnp.concatenate([square_high, square_high], axis=0),
    ) + dot(turned_high, square_low)
    gram_high, gram_low = split(1.0 + cross + 0.5 * (cross * cross + squares))
    gram_ref[0] = gram_high
    gram_ref[1] = gram_low

    def times_gram(high, low):
        both = dot(jnp.concatenate([high, low], axis=0), gram_ref[0])
        return both[:order] + both[order:] + dot(high, gram_ref[1])

    rates = sums_ref[1, :order, :] * (1.0 / math.sqrt(snaps))
    rates_high, rates_low = split(rates)
    u = times_gram(rates_high, rates_low)
    m0 = jnp.sum(rates * u, axis=1, keepdims=True)
    shift = jnp.sum(u * u, axis=1, keepdims=True) / (snaps * m0)
    along = u * (1.0 / snaps) - shift * rates
    along_high, along_low = split(along)
    left_ref[0:order, :] = rates_high
    left_ref[order : 2 * order, :] = along_high
    left_ref[2 * order : 3 * order, :] = rates_low
    left_ref[3 * order : 4 * order, :] = along_low
    on_pair(multiply, 0)
    if spare:
        multiply(2 * pairs * TILE)

    def body(index, carry):
        gather((index - 1) * 2 * TILE, 2 * TILE)
        on_pair(multiply, index)
        on_pair(build, index + 1)
        return carry

    lax.fori_loop(1, pairs - 1, body, 0)
    gather((pairs - 2) * 2 * TILE, 2 * TILE)
    on_pair(multiply, pairs - 1)
    if spare:
        gather(2 * pairs * TILE, TILE)
    gather((pairs - 1) * 2 * TILE, 2 * TILE)

    total = [jnp.sum(acc_ref[k], axis=1, keepdims=True) for k in range(4)]
    bb_extra, ss, ss_extra, bs_extra = total
    ratio = bb_extra / m0
    alpha0 = 1.0 / (shift + mean + ratio)
    perp = ss - ratio * bb_extra
    image = times_gram(along_high, along_low) + v_ref[...] - ratio * u
    energy = (
        jnp.sum(image * image, axis=1, keepdims=True) * (1.0 / snaps)
        + mean * perp
        + ss_extra
        - 2.0 * ratio * bs_extra
        + ratio * ratio * bb_extra
    )
    rr1 = alpha0 * alpha0 * perp
    beta = rr1 / m0
    alpha1 = rr1 / (alpha0 * alpha0 * energy - rr1 * beta / alpha0)
    mix_ref[0] = jnp.broadcast_to(alpha0 + alpha1 * (beta + alpha0 * ratio), (order, LANES))
    mix_ref[1] = jnp.broadcast_to(-alpha1 * alpha0, (order, LANES))

    def copy(group):
        rows = pl.ds(pl.multiple_of(group * 8, 8), 8)
        return pltpu.make_async_copy(x_ref.at[rows, :], out_ref.at[rows, :], sems.at[group])

    def combine(group, carry):
        rows = pl.ds(pl.multiple_of(group * 8, 8), 8)
        on_b = mix_ref[0, rows, :]
        on_s = mix_ref[1, rows, :]
        for left in range(0, width, LANES):
            here = slice(left, min(left + LANES, width))
            size = here.stop - here.start
            x_ref[rows, here] = on_b[:, :size] * b_ref[rows, here] + on_s[:, :size] * s_ref[rows, here]
        copy(group).start()
        return carry

    def finish(group, carry):
        copy(group).wait()
        return carry

    lax.fori_loop(0, order // 8, combine, 0)
    lax.fori_loop(0, order // 8, finish, 0)


def on_device(basis, snapshots, derivatives, quad_pairs, penalty):
    axes = ("gx", "gy")
    devices = lax.axis_size("gx") * lax.axis_size("gy")
    length, order = basis.shape
    snaps = snapshots.shape[1]
    steps = length // TILE if length % TILE == 0 else 1
    count = quad_pairs.shape[1]
    width = 1 + order + count
    padded = round_up(width, TILE)
    assert order + 2 <= LANES and order % 8 == 0
    vmem = pl.BlockSpec(memory_space=pltpu.VMEM)
    part = pl.pallas_call(
        project,
        in_specs=(pl.BlockSpec(memory_space=pltpu.HBM),) * 3,
        out_shape=pltpu.VMEM((2, LANES, snaps), F32),
        out_specs=vmem,
        scratch_shapes=[
            pltpu.VMEM((order, length), BF16),
            pltpu.VMEM((length, snaps), BF16),
            pltpu.VMEM((length, snaps), BF16),
            pltpu.SemaphoreType.DMA((steps, 3)),
        ],
        compiler_params=limit(8),
        name="project",
    )(*(pltpu.with_memory_space_constraint(a, pltpu.HBM) for a in (basis.T, snapshots, derivatives)))
    rows = 2 * LANES
    full = round_up(rows, devices)
    pieces = jnp.pad(part.reshape(rows, snaps), ((0, full - rows), (0, 0)))
    pieces = pieces.reshape(devices, full // devices, snaps)
    pieces = lax.all_to_all(pieces, axes, 0, 0, tiled=True)
    spread = pl.pallas_call(
        add_up,
        out_shape=pltpu.VMEM(pieces.shape, F32),
        out_specs=vmem,
        compiler_params=limit(8),
        name="add_up",
    )(pieces)
    whole = lax.all_to_all(spread, axes, 0, 0, tiled=True)
    sums = whole.reshape(full, snaps)[:rows].reshape(2, LANES, snaps)
    counting = jnp.arange(order, dtype=jnp.int32)
    ones = jnp.full((1 + order,), order, jnp.int32)
    blank = jnp.full((2, padded - width), order + 1, jnp.int32)
    head = jnp.stack([jnp.concatenate([ones[:1], counting]), ones])
    index = jnp.concatenate([head, quad_pairs, blank], axis=1)
    weight = jnp.pad(penalty, (0, padded - width)).reshape(1, padded)
    return pl.pallas_call(
        fit,
        out_shape=jax.ShapeDtypeStruct((order, width), F32),
        in_specs=(vmem,) * 3,
        out_specs=pl.BlockSpec(memory_space=pl.ANY),
        scratch_shapes=[
            pltpu.VMEM((snaps, 2 * LANES), BF16),
            pltpu.VMEM((4 * order, snaps), BF16),
            pltpu.VMEM((2, snaps, snaps), BF16),
            pltpu.VMEM((snaps, padded), BF16),
            pltpu.VMEM((snaps, padded), BF16),
            pltpu.VMEM((order, padded), F32),
            pltpu.VMEM((order, padded), F32),
            pltpu.VMEM((order, snaps), F32),
            pltpu.VMEM((4, order, LANES), F32),
            pltpu.VMEM((1, padded), F32),
            pltpu.VMEM((2, order, LANES), F32),
            pltpu.VMEM((order, width), F32),
            pltpu.SemaphoreType.DMA((order // 8,)),
        ],
        compiler_params=limit(36),
        name="fit",
    )(sums, index, weight)


def solution(mesh):
    split_rows = P(("gx", "gy"), None)
    return jax.shard_map(
        on_device,
        mesh=mesh,
        in_specs=(split_rows, split_rows, split_rows, P(), P()),
        out_specs=P(),
        check_vma=False,
    )
```

time: 61.4 us -> 45.2 us (0.74)
  Pallas kernels: 27.4 us -> 14 us
  local copies, waits for them, and re-layouts: 2.82 us -> 0.97 us
  waiting for transfers between devices: 10.3 us -> 9.57 us
    pallas_call x2 -> x3, Pallas kernels: 27.4 us -> 14 us  [the longest x1 11.4 us: on_device(): pl.pallas_call(fit, out_shape=jax.ShapeDtypeStruct((order, width), F32),...]
    unnamed x7 -> x4, local copies, waits for them, and re-layouts: 1.9 us -> 0.01 us
    pad x1, local copies, waits for them, and re-layouts: 0.01 us -> 0.76 us  [on_device(): weight = jnp.pad(penalty, (0, padded - width)).reshape(1, padded)]
    all_to_all x1, waiting for transfers between devices: 10.3 us -> 9.57 us  [on_device(): whole = lax.all_to_all(spread, axes, 0, 0, tiled=True)]
    broadcast_in_dim x1 -> x0, local copies, waits for them, and re-layouts: 0.72 us -> none  [on_device(): spread = jnp.broadcast_to(summed, pieces.shape)]
  transfers between devices with their start and end apart: 1 -> 1, of which waited for: 1 -> 1; matrix products, arithmetic and copies ran while one was open for 0% -> 2% of each run, Pallas kernels for 0% -> 0%
where the time goes in v2:
time: 45.2 us; the launch traced here: 44.9 us
  blocking collectives  17.7 us (39%)
  Pallas kernels  14 us (31%)
  waiting for transfers between devices  9.57 us (21%)
  starting transfers between devices  2.59 us (6%)
  local copies, waits for them, and re-layouts  0.97 us (2%)
    all_to_all x1, blocking collectives, on_device(): pieces = lax.all_to_all(pieces, axes, 0, 0, tiled=True)  17.7 us
    pallas_call x1, Pallas kernels, on_device(): pl.pallas_call(fit, out_shape=jax.ShapeDtypeStruct((order, width), F32),...  11.4 us
    all_to_all x1, waiting for transfers between devices, on_device(): whole = lax.all_to_all(spread, axes, 0, 0, tiled=True)  9.57 us
    all_to_all x1, starting transfers between devices, on_device(): whole = lax.all_to_all(spread, axes, 0, 0, tiled=True)  2.59 us
    pallas_call x1, Pallas kernels, on_device(): pl.pallas_call(project, in_specs=(pl.BlockSpec(memory_space=pltpu.HBM),)...  1.81 us
  transfers between devices with their start and end apart: 1, of which 1 were waited for; matrix products, arithmetic and copies ran while one was open for 2% of the time, Pallas kernels for 0%

profile of v2, /device:TPU:0, one launch (start us, length us, event | category | flops | bytes accessed | tf_op | source)
XLA Modules:
  0.0 44.9 jit_solution(15977244953486826488)
XLA Ops:
  0.0 0.0 copy-start.1
  0.0 0.0 copy-start
  0.0 1.8 %project.1 = f32[2,128,256]{2,1,0:T(8,128)S(1)} custom-call(bf16[120,1280]{1,0:T(8,128)(2,1)} %bitcast.5, bf16[1280,256]{1,0:T(8,128)(2,1)} %snaps_ref.1, bf16[1280,256]{1,0:T(8,128)(2,1)} %rates_ref.1), custom_call_target="tpu_custom_call" | custom-call | tf_op jit(solution)/shard_map/project/pallas_call | solution.py:224
  1.8 17.7 %all_to_all.10.parts_ref = f32[32,8,256]{2,1,0:T(8,128)S(1)} all-to-all(f32[32,8,256]{2,1,0:T(8,128)S(1)} %bitcast.4), channel_id=1, replica_groups=mesh['gx'=8,'gy'=4] {'gx','gy'}, dimensions={0} | all-to-all | bytes 524288 | tf_op jit(solution)/shard_map/all_to_all | solution.py:242
  19.6 0.8 %add_up.1 = f32[32,8,256]{2,1,0:T(8,128)} custom-call(f32[32,8,256]{2,1,0:T(8,128)S(1)} %all_to_all.10.parts_ref), custom_call_target="tpu_custom_call" | custom-call | tf_op jit(solution)/shard_map/add_up/pallas_call | solution.py:243
  20.3 2.6 %all-to-all-start.1 = ((f32[32,8,256]{2,1,0:T(8,128)}), f32[32,8,256]{2,1,0:T(8,128)S(1)}, u32[]{:S(2)}, u32[]{:S(2)}) async-start(f32[32,8,256]{2,1,0:T(8,128)} %add_up.1), calls=%async_computation.1 | async-start | bytes 524288 | tf_op jit(solution)/shard_map/all_to_all | solution.py:250
  22.9 0.8 %pad.5 = f32[7424]{0:T(1024)S(1)} pad(f32[7381]{0:T(1024)} %param.9, f32[]{:T(128)} %constant.10.clone.1), padding=0_43 | pad | bytes 59224 | tf_op jit(solution)/shard_map/jit(_pad)/pad | solution.py:257
  23.7 0.0 copy-done.1
  23.7 0.0 copy-done
  23.7 0.2 concatenate.4.index_ref
  23.9 9.6 %all-to-all-done.1 = f32[32,8,256]{2,1,0:T(8,128)S(1)} async-done(((f32[32,8,256]{2,1,0:T(8,128)}), f32[32,8,256]{2,1,0:T(8,128)S(1)}, u32[]{:S(2)}, u32[]{:S(2)}) %all-to-all-start.1) | async-done | bytes 262176 | tf_op jit(solution)/shard_map/all_to_all | solution.py:250
  33.5 11.4 %fit.1 = f32[120,7381]{1,0:T(8,128)} custom-call(f32[2,128,256]{2,1,0:T(8,128)S(1)} %bitcast.3, s32[2,7424]{1,0:T(2,128)S(1)} %concatenate.4.index_ref, f32[1,7424]{1,0:T(1,128)S(1)} %reshape.9.weight_ref), custom_call_target="tpu_custom_call" | custom-call | tf_op jit(solution)/shard_map/fit/pallas_call | solution.py:258
  (2 shorter events, 0.0 us)
Async XLA Ops:
  0.0 23.7 %copy-start.1 = (s32[2,121]{1,0:T(2,128)S(1)}, s32[2,121]{1,0:T(2,128)}, u32[]{:S(2)}) copy-start(s32[2,121]{1,0:T(2,128)} %constant.8.clone.1) | copy-start | bytes 2908
  0.0 23.7 %copy-start = (s32[2,7260]{1,0:T(2,128)S(1)}, s32[2,7260]{1,0:T(2,128)}, u32[]{:S(2)}) copy-start(s32[2,7260]{1,0:T(2,128)} %param.8) | copy-start | bytes 174244
  20.3 13.2 %all-to-all-start.1 = ((f32[32,8,256]{2,1,0:T(8,128)}), f32[32,8,256]{2,1,0:T(8,128)S(1)}, u32[]{:S(2)}, u32[]{:S(2)}) async-start(f32[32,8,256]{2,1,0:T(8,128)} %add_up.1), calls=%async_computation.1 | async-start | bytes 524288 | tf_op jit(solution)/shard_map/all_to_all | solution.py:250

commit v3 on v2

--- a/solution.py
+++ b/solution.py
@@ -31,7 +31,7 @@
     return high, (value - high.astype(F32)).astype(BF16)
 
 
-def project(basis_ref, snaps_ref, rates_ref, out_ref, basis_buf, snaps_buf, rates_buf, sems):
+def project(core_ref, basis_ref, snaps_ref, rates_ref, mine_ref, other_ref, basis_buf, snaps_buf, rates_buf, sems):
     order = basis_ref.shape[0]
     count, size = sems.shape[0], snaps_buf.shape[0] // sems.shape[0]
     copies = []
@@ -52,64 +52,84 @@
         here = slice(k * size, (k + 1) * size)
         basis = basis_buf[:, here]
         total = [t + dot(basis, buf[here, :]) for t, buf in zip(total, (snaps_buf, rates_buf))]
+    blank = jnp.zeros((LANES - order, mine_ref.shape[2]), F32)
+    first = core_ref[0] == 0
     for k in range(2):
-        out_ref[k, :order, :] = total[k]
-        out_ref[k, order:, :] = jnp.zeros((LANES - order, out_ref.shape[2]), F32)
+        left, right = jnp.split(total[k], 2, axis=1)
+        mine_ref[k, :order, :] = jnp.where(first, left, right)
+        other_ref[k, :order, :] = jnp.where(first, right, left)
+        mine_ref[k, order:, :] = blank
+        other_ref[k, order:, :] = blank
 
 
 def add_up(parts_ref, out_ref):
-    out_ref[...] = jnp.broadcast_to(jnp.sum(parts_ref[...], axis=0, keepdims=True), out_ref.shape)
+    devices = parts_ref.shape[0]
+    for kind in range(2):
+        total = parts_ref[kind]
+        for k in range(kind + 2, devices, 2):
+            total += parts_ref[k]
+        for k in range(kind, devices, 2):
+            out_ref[k] = total
+
+
+def one_hot(index_ref, k, here):
+    row = lax.broadcasted_iota(jnp.int32, (LANES, TILE), 0)
+    return jnp.where(row == index_ref[k : k + 1, here], 1.0, 0.0).astype(BF16)
 
 
 def fit(
-    sums_ref, index_ref, weight_ref, out_ref,
-    table_ref, left_ref, gram_ref, high_ref, low_ref, b_ref, s_ref, v_ref, acc_ref, extra_ref, mix_ref, x_ref, sems,
+    core_ref, mine_ref, other_ref, index_ref, weight_ref, out_ref,
+    table_ref, left_ref, gram_ref, even_ref, odd_ref, rest_ref, b_ref, s_ref, v_ref, acc_ref, extra_ref, mix_ref, x_ref, sems,
 ):
     order, width = out_ref.shape
-    snaps = sums_ref.shape[2]
+    snaps = 2 * mine_ref.shape[2]
     padded = index_ref.shape[1]
-    pairs = padded // (2 * TILE)
+    pairs = padded // (4 * TILE) * 2
     spare = padded // TILE - 2 * pairs
 
     def place(start, size):
         return pl.ds(start if isinstance(start, int) else pl.multiple_of(start, TILE), size)
 
-    def build(start):
-        here = place(start, TILE)
-        row = lax.broadcasted_iota(jnp.int32, (LANES, TILE), 0)
-        factors = []
-        for k in range(2):
-            hot = jnp.where(row == index_ref[k : k + 1, here], 1.0, 0.0).astype(BF16)
-            factors.append(dot(table_ref[...], jnp.concatenate([hot, hot], axis=0)))
-        high, low = split(factors[0] * factors[1])
-        high_ref[:, here] = high
-        low_ref[:, here] = low
-
-    def multiply(start):
-        here = place(start, TILE)
-        one = dot(left_ref[...], high_ref[:, here])
-        two = dot(left_ref[0 : 2 * order, :], low_ref[:, here])
-        both = one[: 2 * order] + one[2 * order :] + two
-        b = both[:order]
-        b_ref[:, here] = b
-        s_ref[:, here] = both[order:] + extra_ref[0:1, here] * b
-
-    def gather(start, size):
-        here = place(start, size)
-        b = b_ref[:, here]
-        s = s_ref[:, here]
-        extra = extra_ref[0:1, here]
-        scaled = extra * b
-        v_ref[...] += dot(scaled.astype(BF16), high_ref[:, here], ((1,), (1,)))
-        square = s * s
-        for k, term in enumerate((scaled * b, square, extra * square, scaled * s)):
-            acc_ref[k] += sum(term[:, i : i + LANES] for i in range(0, size, LANES))
-
-    def on_pair(stage, index):
-        for half in range(2):
-            stage((2 * index + half) * TILE)
-
-    coeffs = sums_ref[0]
+    def build(data_ref, start, size):
+        for left in range(0, size, TILE):
+            here = place(start + left, TILE)
+            factors = []
+            for k in range(2):
+                hot = one_hot(index_ref, k, here)
+                factors.append(dot(table_ref[...], jnp.concatenate([hot, hot], axis=0)))
+            high, low = split(factors[0] * factors[1])
+            data_ref[0, :, left : left + TILE] = high
+            data_ref[1, :, left : left + TILE] = low
+
+    def multiply(data_ref, start, size):
+        weighted = []
+        terms = [0.0] * 4
+        for left in range(0, size, TILE):
+            here = place(start + left, TILE)
+            high = data_ref[0, :, left : left + TILE]
+            one = dot(left_ref[...], high)
+            two = dot(left_ref[0 : 2 * order, :], data_ref[1, :, left : left + TILE])
+            both = one[: 2 * order] + one[2 * order :] + two
+            extra = extra_ref[0:1, here]
+            b = both[:order]
+            scaled = extra * b
+            s = both[order:] + scaled
+            b_ref[:, here] = b
+            s_ref[:, here] = s
+            weighted.append(scaled.astype(BF16))
+            square = s * s
+            new = (scaled * b, square, extra * square, scaled * s)
+            terms = [t + n[:, :LANES] + n[:, LANES:] for t, n in zip(terms, new)]
+        v_ref[...] += dot(jnp.concatenate(weighted, axis=1), data_ref[0], ((1,), (1,)))
+        for k in range(4):
+            acc_ref[k] += terms[k]
+
+    def whole(k):
+        mine, other = mine_ref[k], other_ref[k]
+        first = core_ref[0] == 0
+        return jnp.concatenate([jnp.where(first, mine, other), jnp.where(first, other, mine)], axis=1)
+
+    coeffs = whole(0)
     coeffs_high, coeffs_low = split(coeffs)
     high, low = split(jnp.transpose(coeffs))
     lane = lax.broadcasted_iota(jnp.int32, (snaps, LANES), 1)
@@ -119,10 +139,10 @@
     extra_ref[...] = weight_ref[...] - mean
     v_ref[...] = jnp.zeros_like(v_ref)
     acc_ref[...] = jnp.zeros_like(acc_ref)
-    on_pair(build, 0)
-    on_pair(build, 1)
+    wide = 2 * TILE
+    build(even_ref, 0, wide)
     if spare:
-        build(2 * pairs * TILE)
+        build(rest_ref, pairs * wide, spare * TILE)
     table = table_ref[...]
     cross = dot(table, jnp.concatenate([coeffs_high, coeffs_high], axis=0)) + dot(high, coeffs_low)
     square = coeffs * coeffs
@@ -140,7 +160,7 @@
         both = dot(jnp.concatenate([high, low], axis=0), gram_ref[0])
         return both[:order] + both[order:] + dot(high, gram_ref[1])
 
-    rates = sums_ref[1, :order, :] * (1.0 / math.sqrt(snaps))
+    rates = whole(1)[:order] * (1.0 / math.sqrt(snaps))
     rates_high, rates_low = split(rates)
     u = times_gram(rates_high, rates_low)
     m0 = jnp.sum(rates * u, axis=1, keepdims=True)
@@ -151,22 +171,21 @@
     left_ref[order : 2 * order, :] = along_high
     left_ref[2 * order : 3 * order, :] = rates_low
     left_ref[3 * order : 4 * order, :] = along_low
-    on_pair(multiply, 0)
     if spare:
-        multiply(2 * pairs * TILE)
-
-    def body(index, carry):
-        gather((index - 1) * 2 * TILE, 2 * TILE)
-        on_pair(multiply, index)
-        on_pair(build, index + 1)
+        multiply(rest_ref, pairs * wide, spare * TILE)
+
+    def body(step, carry):
+        first = 2 * step
+        build(odd_ref, (first + 1) * wide, wide)
+        multiply(even_ref, first * wide, wide)
+        build(even_ref, (first + 2) * wide, wide)
+        multiply(odd_ref, (first + 1) * wide, wide)
         return carry
 
-    lax.fori_loop(1, pairs - 1, body, 0)
-    gather((pairs - 2) * 2 * TILE, 2 * TILE)
-    on_pair(multiply, pairs - 1)
-    if spare:
-        gather(2 * pairs * TILE, TILE)
-    gather((pairs - 1) * 2 * TILE, 2 * TILE)
+    lax.fori_loop(0, pairs // 2 - 1, body, 0)
+    build(odd_ref, (pairs - 1) * wide, wide)
+    multiply(even_ref, (pairs - 2) * wide, wide)
+    multiply(odd_ref, (pairs - 1) * wide, wide)
 
     total = [jnp.sum(acc_ref[k], axis=1, keepdims=True) for k in range(4)]
     bb_extra, ss, ss_extra, bs_extra = total
@@ -219,13 +238,18 @@
     count = quad_pairs.shape[1]
     width = 1 + order + count
     padded = round_up(width, TILE)
-    assert order + 2 <= LANES and order % 8 == 0
+    assert order + 2 <= LANES and order % 8 == 0 and snaps % (2 * LANES) == 0
+    assert lax.axis_size("gy") % 2 == 0
     vmem = pl.BlockSpec(memory_space=pltpu.VMEM)
-    part = pl.pallas_call(
+    smem = pl.BlockSpec(memory_space=pltpu.SMEM)
+    lanes = snaps // 2
+    core = (lax.axis_index("gy") % 2).reshape(1)
+    pair = [(k, k ^ 1) for k in range(lax.axis_size("gy"))]
+    mine, other = pl.pallas_call(
         project,
-        in_specs=(pl.BlockSpec(memory_space=pltpu.HBM),) * 3,
-        out_shape=pltpu.VMEM((2, LANES, snaps), F32),
-        out_specs=vmem,
+        in_specs=(smem,) + (pl.BlockSpec(memory_space=pltpu.HBM),) * 3,
+        out_shape=(pltpu.VMEM((2, LANES, lanes), F32),) * 2,
+        out_specs=(vmem,) * 2,
         scratch_shapes=[
             pltpu.VMEM((order, length), BF16),
             pltpu.VMEM((length, snaps), BF16),
@@ -234,11 +258,12 @@
         ],
         compiler_params=limit(8),
         name="project",
-    )(*(pltpu.with_memory_space_constraint(a, pltpu.HBM) for a in (basis.T, snapshots, derivatives)))
+    )(core, *(pltpu.with_memory_space_constraint(a, pltpu.HBM) for a in (basis.T, snapshots, derivatives)))
+    mine = mine + lax.ppermute(other, "gy", pair)
     rows = 2 * LANES
     full = round_up(rows, devices)
-    pieces = jnp.pad(part.reshape(rows, snaps), ((0, full - rows), (0, 0)))
-    pieces = pieces.reshape(devices, full // devices, snaps)
+    pieces = jnp.pad(mine.reshape(rows, lanes), ((0, full - rows), (0, 0)))
+    pieces = pieces.reshape(devices, full // devices, lanes)
     pieces = lax.all_to_all(pieces, axes, 0, 0, tiled=True)
     spread = pl.pallas_call(
         add_up,
@@ -247,8 +272,9 @@
         compiler_params=limit(8),
         name="add_up",
     )(pieces)
-    whole = lax.all_to_all(spread, axes, 0, 0, tiled=True)
-    sums = whole.reshape(full, snaps)[:rows].reshape(2, LANES, snaps)
+    half = lax.all_to_all(spread, axes, 0, 0, tiled=True)
+    half = half.reshape(full, lanes)[:rows].reshape(2, LANES, lanes)
+    rest = lax.ppermute(half, "gy", pair)
     counting = jnp.arange(order, dtype=jnp.int32)
     ones = jnp.full((1 + order,), order, jnp.int32)
     blank = jnp.full((2, padded - width), order + 1, jnp.int32)
@@ -258,14 +284,15 @@
     return pl.pallas_call(
         fit,
         out_shape=jax.ShapeDtypeStruct((order, width), F32),
-        in_specs=(vmem,) * 3,
+        in_specs=(smem,) + (vmem,) * 4,
         out_specs=pl.BlockSpec(memory_space=pl.ANY),
         scratch_shapes=[
             pltpu.VMEM((snaps, 2 * LANES), BF16),
             pltpu.VMEM((4 * order, snaps), BF16),
             pltpu.VMEM((2, snaps, snaps), BF16),
-            pltpu.VMEM((snaps, padded), BF16),
-            pltpu.VMEM((snaps, padded), BF16),
+            pltpu.VMEM((2, snaps, 2 * TILE), BF16),
+            pltpu.VMEM((2, snaps, 2 * TILE), BF16),
+            pltpu.VMEM((2, snaps, max(padded // TILE % 4, 1) * TILE), BF16),
             pltpu.VMEM((order, padded), F32),
             pltpu.VMEM((order, padded), F32),
             pltpu.VMEM((order, snaps), F32),
@@ -277,7 +304,7 @@
         ],
         compiler_params=limit(36),
         name="fit",
-    )(sums, index, weight)
+    )(core, half, rest, index, weight)
 
 
 def solution(mesh):

time: 45.2 us -> 41.9 us (0.927)
  waiting for transfers between devices: 9.57 us -> 0.99 us
  blocking collectives: 17.7 us -> 25.2 us
  starting transfers between devices: 2.59 us -> 0.77 us
  Pallas kernels: 14 us -> 12.8 us
  local copies, waits for them, and re-layouts: 0.97 us -> 1.79 us
    all_to_all x0 -> x1, blocking collectives: none -> 9.97 us  [on_device(): half = lax.all_to_all(spread, axes, 0, 0, tiled=True)]
    all_to_all x1 -> x0, waiting for transfers between devices: 9.57 us -> none  [on_device(): whole = lax.all_to_all(spread, axes, 0, 0, tiled=True)]
    all_to_all x1 -> x0, starting transfers between devices: 2.59 us -> none  [on_device(): whole = lax.all_to_all(spread, axes, 0, 0, tiled=True)]
    all_to_all x1, blocking collectives: 17.7 us -> 15.2 us  [on_device(): pieces = lax.all_to_all(pieces, axes, 0, 0, tiled=True)]
    ppermute x0 -> x2, waiting for transfers between devices: none -> 0.99 us  [the longest x1 0.99 us: on_device(): mine = mine + lax.ppermute(other, 'gy', pair)]
    concatenate x1, local copies, waits for them, and re-layouts: 0.18 us -> 1.01 us  [on_device(): index = jnp.concatenate([head, quad_pairs, blank], axis=1)]
    ppermute x0 -> x2, starting transfers between devices: none -> 0.77 us  [the longest x1 0.56 us: on_device(): mine = mine + lax.ppermute(other, 'gy', pair)]
    pallas_call x1, Pallas kernels: 0.75 us -> 0.03 us  [on_device(): pl.pallas_call(add_up, out_shape=pltpu.VMEM(pieces.shape, F32), out_specs...]
  transfers between devices with their start and end apart: 1 -> 2, of which waited for: 1 -> 1; matrix products, arithmetic and copies ran while one was open for 2% -> 4% of each run, Pallas kernels for 0% -> 0%
where the time goes in v3:
time: 41.9 us; the launch traced here: 41.6 us
  blocking collectives  25.2 us (60%)
  Pallas kernels  12.8 us (31%)
  local copies, waits for them, and re-layouts  1.79 us (4%)
  waiting for transfers between devices  0.99 us (2%)
  starting transfers between devices  0.77 us (2%)
    all_to_all x1, blocking collectives, on_device(): pieces = lax.all_to_all(pieces, axes, 0, 0, tiled=True)  15.2 us
    pallas_call x1, Pallas kernels, on_device(): pl.pallas_call(fit, out_shape=jax.ShapeDtypeStruct((order, width), F32),...  10.9 us
    all_to_all x1, blocking collectives, on_device(): half = lax.all_to_all(spread, axes, 0, 0, tiled=True)  9.97 us
    pallas_call x1, Pallas kernels, on_device(): pl.pallas_call(project, in_specs=(smem,) + (pl.BlockSpec(memory_space=plt...  1.8 us
    concatenate x1, local copies, waits for them, and re-layouts, on_device(): index = jnp.concatenate([head, quad_pairs, blank], axis=1)  1.01 us
    ppermute x1, waiting for transfers between devices, on_device(): mine = mine + lax.ppermute(other, 'gy', pair)  0.99 us
  transfers between devices with their start and end apart: 2, of which 1 were waited for; matrix products, arithmetic and copies ran while one was open for 4% of the time, Pallas kernels for 0%

profile of v3, /device:TPU:0, one launch (start us, length us, event | category | flops | bytes accessed | tf_op | source)
XLA Modules:
  0.0 41.6 jit_solution(15450745802696224475)
XLA Ops:
  0.0 1.8 %project.1 = (f32[2,128,128]{2,1,0:T(8,128)S(1)}, f32[2,128,128]{2,1,0:T(8,128)S(1)}) custom-call(s32[1]{0:T(128)} %bitcast.core_ref, bf16[120,1280]{1,0:T(8,128)(2,1)} %bitcast.7, bf16[1280,256]{1,0:T(8,128)(2,1)} %snaps_ref.1, bf16[1280,256]{1,0:T(8,128)(2,1)} %rates_ref.1), custom_call_target="tpu_custom_call" | custom-call | tf_op jit(solution)/shard_map/project/pallas_call | solution.py:248
  1.8 0.6 %collective-permute-start = (f32[2,128,128]{2,1,0:T(8,128)S(1)}, f32[2,128,128]{2,1,0:T(8,128)S(1)}, u32[]{:S(2)}, u32[]{:S(2)}) collective-permute-start(f32[2,128,128]{2,1,0:T(8,128)S(1)} %get-tuple-element.8), channel_id=1, source_target_pairs={{0,1},{1,0},{2,3},{3,2},{4,5},{5,4},{6,7},{7,6},{8,9},{9,8},{10,11... | collective-permute-start | bytes 393224 | tf_op jit(solution)/shard_map/ppermute | solution.py:262
  2.4 1.0 %collective-permute-done = f32[2,128,128]{2,1,0:T(8,128)S(1)} collective-permute-done((f32[2,128,128]{2,1,0:T(8,128)S(1)}, f32[2,128,128]{2,1,0:T(8,128)S(1)}, u32[]{:S(2)}, u32[]{:S(2)}) %collective-permute-start) | collective-permute-done | bytes 131104 | tf_op jit(solution)/shard_map/ppermute | solution.py:262
  3.4 15.2 %all_to_all.10.parts_ref = f32[32,8,128]{2,1,0:T(8,128)S(1)} all-to-all(f32[32,8,128]{2,1,0:T(8,128)S(1)} %bitcast.6), channel_id=1, replica_groups=mesh['gx'=8,'gy'=4] {'gx','gy'}, dimensions={0} | all-to-all | bytes 262144 | tf_op jit(solution)/shard_map/all_to_all | solution.py:267
  18.6 10.0 %all_to_all.11 = f32[32,8,128]{2,1,0:T(8,128)S(1)} all-to-all(f32[32,8,128]{2,1,0:T(8,128)S(1)} %add_up.1), channel_id=1, replica_groups=mesh['gx'=8,'gy'=4] {'gx','gy'}, dimensions={0} | all-to-all | bytes 262144 | tf_op jit(solution)/shard_map/all_to_all | solution.py:275
  28.6 0.2 collective-permute-start.1
  28.8 0.8 %pad.5 = f32[7424]{0:T(1024)S(1)} pad(f32[7381]{0:T(1024)} %param.9, f32[]{:T(128)} %constant.27.clone.1), padding=0_43 | pad | bytes 59224 | tf_op jit(solution)/shard_map/jit(_pad)/pad | solution.py:283
  29.6 1.0 %concatenate.4.index_ref = s32[2,7424]{1,0:T(2,128)S(1)} concatenate(s32[2,121]{1,0:T(2,128)} %constant.25.clone.1, s32[2,7260]{1,0:T(2,128)} %param.8, s32[2,43]{1,0:T(2,128)S(1)} %broadcast_in_dim.3), dimensions={1} | concatenate | bytes 118784 | tf_op jit(solution)/shard_map/concatenate | solution.py:282
  30.6 0.0 collective-permute-done.1.other_ref
  30.6 10.9 %fit.1 = f32[120,7381]{1,0:T(8,128)} custom-call(s32[1]{0:T(128)} %bitcast.core_ref, f32[2,128,128]{2,1,0:T(8,128)S(1)} %bitcast.5, f32[2,128,128]{2,1,0:T(8,128)S(1)} %collective-permute-done.1.other_ref, s32[2,7424]{1,0:T(2,128)S(1)} %concatenate.4.index_ref, f32[1,7424]{1,0:T(1,128)S(1)} %reshape.13.weight_ref), custom_call_target="tpu_custom_call" | custom-call | tf_op jit(solution)/shard_map/fit/pallas_call | solution.py:284
  (4 shorter events, 0.1 us)
Async XLA Ops:
  1.8 1.5 %collective-permute-start = (f32[2,128,128]{2,1,0:T(8,128)S(1)}, f32[2,128,128]{2,1,0:T(8,128)S(1)}, u32[]{:S(2)}, u32[]{:S(2)}) collective-permute-start(f32[2,128,128]{2,1,0:T(8,128)S(1)} %get-tuple-element.8), channel_id=1, source_target_pairs={{0,1},{1,0},{2,3},{3,2},{4,5},{5,4},{6,7},{7,6},{8,9},{9,8},{10,11... | collective-permute-start | bytes 393224 | tf_op jit(solution)/shard_map/ppermute | solution.py:262
  28.6 2.0 %collective-permute-start.1 = (f32[2,128,128]{2,1,0:T(8,128)S(1)}, f32[2,128,128]{2,1,0:T(8,128)S(1)}, u32[]{:S(2)}, u32[]{:S(2)}) collective-permute-start(f32[2,128,128]{2,1,0:T(8,128)S(1)} %bitcast.4), channel_id=1, source_target_pairs={{0,1},{1,0},{2,3},{3,2},{4,5},{5,4},{6,7},{7,6},{8,9},{9,8},{10,11... | collective-permute-start | bytes 393224 | tf_op jit(solution)/shard_map/ppermute | solution.py:277

commit v4 on v3

--- a/solution.py
+++ b/solution.py
@@ -31,7 +31,7 @@
     return high, (value - high.astype(F32)).astype(BF16)
 
 
-def project(core_ref, basis_ref, snaps_ref, rates_ref, mine_ref, other_ref, basis_buf, snaps_buf, rates_buf, sems):
+def project(core_ref, basis_ref, snaps_ref, rates_ref, pairs_ref, mine_ref, other_ref, held_ref, basis_buf, snaps_buf, rates_buf, sems, pair_sem):
     order = basis_ref.shape[0]
     count, size = sems.shape[0], snaps_buf.shape[0] // sems.shape[0]
     copies = []
@@ -45,6 +45,8 @@
         for copy in mine:
             copy.start()
         copies.append(mine)
+    hold = pltpu.make_async_copy(pairs_ref, held_ref, pair_sem)
+    hold.start()
     total = [0.0, 0.0]
     for k in range(count):
         for copy in copies[k]:
@@ -60,6 +62,7 @@
         other_ref[k, :order, :] = jnp.where(first, right, left)
         mine_ref[k, order:, :] = blank
         other_ref[k, order:, :] = blank
+    hold.wait()
 
 
 def add_up(parts_ref, out_ref):
@@ -72,20 +75,57 @@
             out_ref[k] = total
 
 
-def one_hot(index_ref, k, here):
-    row = lax.broadcasted_iota(jnp.int32, (LANES, TILE), 0)
-    return jnp.where(row == index_ref[k : k + 1, here], 1.0, 0.0).astype(BF16)
+def one_hot(index):
+    group = 16
+    wanted = jnp.broadcast_to(index, (group, index.shape[1])).astype(BF16)
+    row = lax.broadcasted_iota(jnp.int32, wanted.shape, 0).astype(F32)
+    one, zero = jnp.ones(wanted.shape, BF16), jnp.zeros(wanted.shape, BF16)
+    parts = [jnp.where((row + top).astype(BF16) == wanted, one, zero) for top in range(0, LANES, group)]
+    return jnp.concatenate(parts, axis=0)
+
+
+def product(table, hots):
+    first, second = (dot(table, jnp.concatenate([hot, hot], axis=0)) for hot in hots)
+    return split(first * second)
+
+
+def make_table(coeffs, order):
+    high, low = split(jnp.transpose(coeffs))
+    lane = lax.broadcasted_iota(jnp.int32, high.shape, 1)
+    high = jnp.where(lane == order, 1.0, high.astype(F32)).astype(BF16)
+    return jnp.concatenate([high, low], axis=1)
+
+
+def begin(order, width, mine_ref, pairs_ref, ready_ref, hot_ref, table_ref, index_ref):
+    table_ref[...] = make_table(mine_ref[0], order)
+    table = table_ref[...]
+    padded = index_ref.shape[1]
+    index_ref[0:2, : pairs_ref.shape[1]] = pairs_ref[...]
+    turned = pltpu.roll(index_ref[...], order + 1, axis=1)
+    row = lax.broadcasted_iota(jnp.int32, turned.shape, 0)
+    lane = lax.broadcasted_iota(jnp.int32, turned.shape, 1)
+    linear = jnp.where((row == 0) & (lane > 0), lane - 1, order)
+    index_ref[...] = jnp.where(lane <= order, linear, jnp.where(lane < width, turned, order + 1))
+    for left in range(0, padded, TILE):
+        here = slice(left, left + TILE)
+        index = index_ref[:, here].astype(F32)
+        hots = [one_hot(index[k : k + 1]) for k in range(2)]
+        for k in range(2):
+            hot_ref[k, :, here] = hots[k]
+        ready_ref[0, :, here], ready_ref[1, :, here] = product(table, hots)
 
 
 def fit(
-    core_ref, mine_ref, other_ref, index_ref, weight_ref, out_ref,
-    table_ref, left_ref, gram_ref, even_ref, odd_ref, rest_ref, b_ref, s_ref, v_ref, acc_ref, extra_ref, mix_ref, x_ref, sems,
+    core_ref, mine_ref, other_ref, ready_ref, hot_ref, own_ref, weight_ref, out_ref,
+    far_ref, table_ref, left_ref, gram_ref, even_ref, odd_ref, rest_ref, b_ref, s_ref, v_ref, acc_ref, extra_ref, mix_ref, x_ref, sems,
 ):
     order, width = out_ref.shape
-    snaps = 2 * mine_ref.shape[2]
-    padded = index_ref.shape[1]
+    lanes = mine_ref.shape[2]
+    snaps = 2 * lanes
+    padded = hot_ref.shape[2]
     pairs = padded // (4 * TILE) * 2
     spare = padded // TILE - 2 * pairs
+    core = core_ref[0]
 
     def place(start, size):
         return pl.ds(start if isinstance(start, int) else pl.multiple_of(start, TILE), size)
@@ -93,22 +133,22 @@
     def build(data_ref, start, size):
         for left in range(0, size, TILE):
             here = place(start + left, TILE)
-            factors = []
+            there = slice(left, left + TILE)
+            parts = product(far_ref[...], [hot_ref[k, :, here] for k in range(2)])
             for k in range(2):
-                hot = one_hot(index_ref, k, here)
-                factors.append(dot(table_ref[...], jnp.concatenate([hot, hot], axis=0)))
-            high, low = split(factors[0] * factors[1])
-            data_ref[0, :, left : left + TILE] = high
-            data_ref[1, :, left : left + TILE] = low
+                data_ref[k, core, :, there] = ready_ref[k, :, here]
+                data_ref[k, 1 - core, :, there] = parts[k]
+
+    def load(data_ref, k, left, size):
+        return data_ref[k, :, :, left : left + size].reshape(snaps, size)
 
     def multiply(data_ref, start, size):
         weighted = []
         terms = [0.0] * 4
         for left in range(0, size, TILE):
             here = place(start + left, TILE)
-            high = data_ref[0, :, left : left + TILE]
-            one = dot(left_ref[...], high)
-            two = dot(left_ref[0 : 2 * order, :], data_ref[1, :, left : left + TILE])
+            one = dot(left_ref[...], load(data_ref, 0, left, TILE))
+            two = dot(left_ref[0 : 2 * order, :], load(data_ref, 1, left, TILE))
             both = one[: 2 * order] + one[2 * order :] + two
             extra = extra_ref[0:1, here]
             b = both[:order]
@@ -120,34 +160,34 @@
             square = s * s
             new = (scaled * b, square, extra * square, scaled * s)
             terms = [t + n[:, :LANES] + n[:, LANES:] for t, n in zip(terms, new)]
-        v_ref[...] += dot(jnp.concatenate(weighted, axis=1), data_ref[0], ((1,), (1,)))
+        v_ref[...] += dot(jnp.concatenate(weighted, axis=1), load(data_ref, 0, 0, size), ((1,), (1,)))
         for k in range(4):
             acc_ref[k] += terms[k]
 
     def whole(k):
         mine, other = mine_ref[k], other_ref[k]
-        first = core_ref[0] == 0
-        return jnp.concatenate([jnp.where(first, mine, other), jnp.where(first, other, mine)], axis=1)
-
-    coeffs = whole(0)
-    coeffs_high, coeffs_low = split(coeffs)
-    high, low = split(jnp.transpose(coeffs))
-    lane = lax.broadcasted_iota(jnp.int32, (snaps, LANES), 1)
-    table_ref[:, :LANES] = jnp.where(lane == order, 1.0, high.astype(F32)).astype(BF16)
-    table_ref[:, LANES:] = low
+        return jnp.concatenate([jnp.where(core == 0, mine, other), jnp.where(core == 0, other, mine)], axis=1)
+
+    far_ref[...] = make_table(other_ref[0], order)
+    table_ref[core] = own_ref[...]
+    table_ref[1 - core] = far_ref[...]
     mean = jnp.sum(weight_ref[...], axis=1, keepdims=True) * (1.0 / width)
-    extra_ref[...] = weight_ref[...] - mean
+    extra_ref[...] = jnp.zeros_like(extra_ref)
+    extra_ref[:, :width] = weight_ref[...] - mean
     v_ref[...] = jnp.zeros_like(v_ref)
     acc_ref[...] = jnp.zeros_like(acc_ref)
     wide = 2 * TILE
     build(even_ref, 0, wide)
     if spare:
         build(rest_ref, pairs * wide, spare * TILE)
-    table = table_ref[...]
+    coeffs = whole(0)
+    coeffs_high, coeffs_low = split(coeffs)
+    table = table_ref[...].reshape(snaps, 2 * LANES)
+    high, low = table[:, :LANES], table[:, LANES:]
     cross = dot(table, jnp.concatenate([coeffs_high, coeffs_high], axis=0)) + dot(high, coeffs_low)
-    square = coeffs * coeffs
-    square_high, square_low = split(square)
-    turned_high, turned_low = split(jnp.transpose(square))
+    square_high, square_low = split(coeffs * coeffs)
+    turned = high.astype(F32) + low.astype(F32)
+    turned_high, turned_low = split(turned * turned)
     squares = dot(
         jnp.concatenate([turned_high, turned_low], axis=1),
         jnp.concatenate([square_high, square_high], axis=0),
@@ -245,21 +285,22 @@
     lanes = snaps // 2
     core = (lax.axis_index("gy") % 2).reshape(1)
     pair = [(k, k ^ 1) for k in range(lax.axis_size("gy"))]
-    mine, other = pl.pallas_call(
+    mine, other, held = pl.pallas_call(
         project,
-        in_specs=(smem,) + (pl.BlockSpec(memory_space=pltpu.HBM),) * 3,
-        out_shape=(pltpu.VMEM((2, LANES, lanes), F32),) * 2,
-        out_specs=(vmem,) * 2,
+        in_specs=(smem,) + (pl.BlockSpec(memory_space=pltpu.HBM),) * 4,
+        out_shape=(pltpu.VMEM((2, LANES, lanes), F32),) * 2 + (pltpu.VMEM(quad_pairs.shape, jnp.int32),),
+        out_specs=(vmem,) * 3,
         scratch_shapes=[
             pltpu.VMEM((order, length), BF16),
             pltpu.VMEM((length, snaps), BF16),
             pltpu.VMEM((length, snaps), BF16),
             pltpu.SemaphoreType.DMA((steps, 3)),
+            pltpu.SemaphoreType.DMA,
         ],
         compiler_params=limit(8),
         name="project",
-    )(core, *(pltpu.with_memory_space_constraint(a, pltpu.HBM) for a in (basis.T, snapshots, derivatives)))
-    mine = mine + lax.ppermute(other, "gy", pair)
+    )(core, *(pltpu.with_memory_space_constraint(a, pltpu.HBM) for a in (basis.T, snapshots, derivatives, quad_pairs)))
+    mine, weight = lax.optimization_barrier((mine + lax.ppermute(other, "gy", pair), penalty.reshape(1, width)))
     rows = 2 * LANES
     full = round_up(rows, devices)
     pieces = jnp.pad(mine.reshape(rows, lanes), ((0, full - rows), (0, 0)))
@@ -275,24 +316,33 @@
     half = lax.all_to_all(spread, axes, 0, 0, tiled=True)
     half = half.reshape(full, lanes)[:rows].reshape(2, LANES, lanes)
     rest = lax.ppermute(half, "gy", pair)
-    counting = jnp.arange(order, dtype=jnp.int32)
-    ones = jnp.full((1 + order,), order, jnp.int32)
-    blank = jnp.full((2, padded - width), order + 1, jnp.int32)
-    head = jnp.stack([jnp.concatenate([ones[:1], counting]), ones])
-    index = jnp.concatenate([head, quad_pairs, blank], axis=1)
-    weight = jnp.pad(penalty, (0, padded - width)).reshape(1, padded)
+    ready, hot, own = pl.pallas_call(
+        lambda *refs: begin(order, width, *refs),
+        in_specs=(vmem,) * 2,
+        out_shape=(
+            pltpu.VMEM((2, lanes, padded), BF16),
+            pltpu.VMEM((2, LANES, padded), BF16),
+            pltpu.VMEM((lanes, 2 * LANES), BF16),
+        ),
+        out_specs=(vmem,) * 3,
+        scratch_shapes=[pltpu.VMEM((8, padded), jnp.int32)],
+        compiler_params=limit(8),
+        cost_estimate=pl.CostEstimate(flops=2 * 10**9, transcendentals=0, bytes_accessed=8 * 10**6),
+        name="begin",
+    )(half, held)
     return pl.pallas_call(
         fit,
         out_shape=jax.ShapeDtypeStruct((order, width), F32),
-        in_specs=(smem,) + (vmem,) * 4,
+        in_specs=(smem,) + (vmem,) * 6,
         out_specs=pl.BlockSpec(memory_space=pl.ANY),
         scratch_shapes=[
-            pltpu.VMEM((snaps, 2 * LANES), BF16),
+            pltpu.VMEM((lanes, 2 * LANES), BF16),
+            pltpu.VMEM((2, lanes, 2 * LANES), BF16),
             pltpu.VMEM((4 * order, snaps), BF16),
             pltpu.VMEM((2, snaps, snaps), BF16),
-            pltpu.VMEM((2, snaps, 2 * TILE), BF16),
-            pltpu.VMEM((2, snaps, 2 * TILE), BF16),
-            pltpu.VMEM((2, snaps, max(padded // TILE % 4, 1) * TILE), BF16),
+            pltpu.VMEM((2, 2, lanes, 2 * TILE), BF16),
+            pltpu.VMEM((2, 2, lanes, 2 * TILE), BF16),
+            pltpu.VMEM((2, 2, lanes, max(padded // TILE % 4, 1) * TILE), BF16),
             pltpu.VMEM((order, padded), F32),
             pltpu.VMEM((order, padded), F32),
             pltpu.VMEM((order, snaps), F32),
@@ -304,7 +354,7 @@
         ],
         compiler_params=limit(36),
         name="fit",
-    )(core, half, rest, index, weight)
+    )(core, half, rest, ready, hot, own, weight)
 
 
 def solution(mesh):

time: 41.9 us -> 40.1 us (0.957)
  local copies, waits for them, and re-layouts: 1.79 us -> 0.78 us
  waiting for transfers between devices: 0.99 us -> 0.21 us
    pallas_call x0 -> x1, Pallas kernels: none -> 1.35 us  [on_device(): pl.pallas_call(lambda *refs: begin(order, width, *refs), in_specs=(vmem,)...]
    pallas_call x1, Pallas kernels: 10.9 us -> 9.72 us  [on_device(): pl.pallas_call(fit, out_shape=jax.ShapeDtypeStruct((order, width), F32),...]
    concatenate x1 -> x0, local copies, waits for them, and re-layouts: 1.01 us -> none  [on_device(): index = jnp.concatenate([head, quad_pairs, blank], axis=1)]
    ppermute x1, waiting for transfers between devices: 0.99 us -> 0.2 us  [on_device(): lax.ppermute(other, 'gy', pair)]
    pad x1 -> x0, local copies, waits for them, and re-layouts: 0.76 us -> none  [on_device(): weight = jnp.pad(penalty, (0, padded - width)).reshape(1, padded)]
    reshape x1, local copies, waits for them, and re-layouts: 0.02 us -> 0.78 us  [on_device(): penalty.reshape(1, width)]
  transfers between devices with their start and end apart: 2 -> 2, of which waited for: 1 -> 1; matrix products, arithmetic and copies ran while one was open for 4% -> 2% of each run, Pallas kernels for 0% -> 3%
where the time goes in v4:
time: 40.1 us; the launch traced here: 39.9 us
  blocking collectives  25.2 us (63%)
  Pallas kernels  12.9 us (32%)
  local copies, waits for them, and re-layouts  0.78 us (2%)
  starting transfers between devices  0.77 us (2%)
    all_to_all x1, blocking collectives, on_device(): pieces = lax.all_to_all(pieces, axes, 0, 0, tiled=True)  15.2 us
    all_to_all x1, blocking collectives, on_device(): half = lax.all_to_all(spread, axes, 0, 0, tiled=True)  9.97 us
    pallas_call x1, Pallas kernels, on_device(): pl.pallas_call(fit, out_shape=jax.ShapeDtypeStruct((order, width), F32),...  9.72 us
    pallas_call x1, Pallas kernels, on_device(): pl.pallas_call(project, in_specs=(smem,) + (pl.BlockSpec(memory_space=plt...  1.81 us
    pallas_call x1, Pallas kernels, on_device(): pl.pallas_call(lambda *refs: begin(order, width, *refs), in_specs=(vmem,)...  1.35 us
  transfers between devices with their start and end apart: 2, of which 1 were waited for; matrix products, arithmetic and copies ran while one was open for 2% of the time, Pallas kernels for 3%

profile of v4, /device:TPU:0, one launch (start us, length us, event | category | flops | bytes accessed | tf_op | source)
XLA Modules:
  0.0 39.9 jit_solution(7306460177060520926)
XLA Ops:
  0.0 1.8 %project.1 = (f32[2,128,128]{2,1,0:T(8,128)S(1)}, f32[2,128,128]{2,1,0:T(8,128)S(1)}, s32[2,7260]{1,0:T(2,128)S(1)}) custom-call(s32[1]{0:T(128)} %bitcast.core_ref, bf16[120,1280]{1,0:T(8,128)(2,1)} %bitcast.8, bf16[1280,256]{1,0:T(8,128)(2,1)} %snaps_ref.1, bf16[1280,256]{1,0:T(8,128)(2,1)} %rates_ref.1, s32[2,7260]{1,0:T(2,128)} %pairs_ref.1), custom_call_target="tpu_custom_call" | custom-call | tf_op jit(solution)/shard_map/project/pallas_call | solution.py:288
  1.8 0.6 %collective-permute-start = (f32[2,128,128]{2,1,0:T(8,128)S(1)}, f32[2,128,128]{2,1,0:T(8,128)S(1)}, u32[]{:S(2)}, u32[]{:S(2)}) collective-permute-start(f32[2,128,128]{2,1,0:T(8,128)S(1)} %get-tuple-element.14), channel_id=1, source_target_pairs={{0,1},{1,0},{2,3},{3,2},{4,5},{5,4},{6,7},{7,6},{8,9},{9,8},{10,11... | collective-permute-start | bytes 393224 | tf_op jit(solution)/shard_map/ppermute | solution.py:303
  2.4 0.8 %reshape.12.weight_ref = f32[1,7381]{1,0:T(1,128)S(1)} reshape(f32[7381]{0:T(1024)} %param.9) | data formatting | bytes 59048 | tf_op jit(solution)/shard_map/reshape | solution.py:303
  3.2 0.2 collective-permute-done
  3.4 15.2 %all_to_all.10.parts_ref = f32[32,8,128]{2,1,0:T(8,128)S(1)} all-to-all(f32[32,8,128]{2,1,0:T(8,128)S(1)} %bitcast.7), channel_id=1, replica_groups=mesh['gx'=8,'gy'=4] {'gx','gy'}, dimensions={0} | all-to-all | bytes 262144 | tf_op jit(solution)/shard_map/all_to_all | solution.py:308
  18.6 10.0 %all_to_all.11 = f32[32,8,128]{2,1,0:T(8,128)S(1)} all-to-all(f32[32,8,128]{2,1,0:T(8,128)S(1)} %add_up.1), channel_id=1, replica_groups=mesh['gx'=8,'gy'=4] {'gx','gy'}, dimensions={0} | all-to-all | bytes 262144 | tf_op jit(solution)/shard_map/all_to_all | solution.py:316
  28.6 0.2 collective-permute-start.1
  28.8 1.4 %begin.1 = (bf16[2,128,7424]{2,1,0:T(8,128)(2,1)S(1)}, bf16[2,128,7424]{2,1,0:T(8,128)(2,1)S(1)}, bf16[128,256]{1,0:T(8,128)(2,1)S(1)}) custom-call(f32[2,128,128]{2,1,0:T(8,128)S(1)} %bitcast.5, s32[2,7260]{1,0:T(2,128)S(1)} %get-tuple-element.16.refs_1_), custom_call_target="tpu_custom_call" | custom-call | flops 2000000000 | bytes 8000000 | tf_op jit(solution)/shard_map/begin/pallas_call | solution.py:319
  30.2 0.0 collective-permute-done.1.other_ref
  30.2 9.7 %fit.1 = f32[120,7381]{1,0:T(8,128)} custom-call(s32[1]{0:T(128)} %bitcast.core_ref, f32[2,128,128]{2,1,0:T(8,128)S(1)} %bitcast.6, f32[2,128,128]{2,1,0:T(8,128)S(1)} %collective-permute-done.1.other_ref, bf16[2,128,7424]{2,1,0:T(8,128)(2,1)S(1)} %get-tuple-element.17.ready_ref, bf16[2,128,7424]{2,1,0:T(8,128)(2,1)S(1)} %get-tuple-element.18.hot_ref, ...), custom_call_target="tpu_custom_call" | custom-call | tf_op jit(solution)/shard_map/fit/pallas_call | solution.py:333
  (2 shorter events, 0.0 us)
Async XLA Ops:
  1.8 1.5 %collective-permute-start = (f32[2,128,128]{2,1,0:T(8,128)S(1)}, f32[2,128,128]{2,1,0:T(8,128)S(1)}, u32[]{:S(2)}, u32[]{:S(2)}) collective-permute-start(f32[2,128,128]{2,1,0:T(8,128)S(1)} %get-tuple-element.14), channel_id=1, source_target_pairs={{0,1},{1,0},{2,3},{3,2},{4,5},{5,4},{6,7},{7,6},{8,9},{9,8},{10,11... | collective-permute-start | bytes 393224 | tf_op jit(solution)/shard_map/ppermute | solution.py:303
  28.6 1.6 %collective-permute-start.1 = (f32[2,128,128]{2,1,0:T(8,128)S(1)}, f32[2,128,128]{2,1,0:T(8,128)S(1)}, u32[]{:S(2)}, u32[]{:S(2)}) collective-permute-start(f32[2,128,128]{2,1,0:T(8,128)S(1)} %bitcast.4), channel_id=1, source_target_pairs={{0,1},{1,0},{2,3},{3,2},{4,5},{5,4},{6,7},{7,6},{8,9},{9,8},{10,11... | collective-permute-start | bytes 393224 | tf_op jit(solution)/shard_map/ppermute | solution.py:318

commit v5 on v4

--- a/solution.py
+++ b/solution.py
@@ -9,6 +9,7 @@
 
 LANES = 128
 TILE = 256
+GROUP = 7
 F32 = jnp.float32
 BF16 = jnp.bfloat16
 ROWS = ((1,), (0,))
@@ -123,8 +124,10 @@
     lanes = mine_ref.shape[2]
     snaps = 2 * lanes
     padded = hot_ref.shape[2]
-    pairs = padded // (4 * TILE) * 2
-    spare = padded // TILE - 2 * pairs
+    wide = GROUP * TILE
+    groups = padded // (2 * wide) * 2
+    spare = padded // TILE - GROUP * groups
+    assert groups >= 2
     core = core_ref[0]
 
     def place(start, size):
@@ -176,10 +179,9 @@
     extra_ref[:, :width] = weight_ref[...] - mean
     v_ref[...] = jnp.zeros_like(v_ref)
     acc_ref[...] = jnp.zeros_like(acc_ref)
-    wide = 2 * TILE
     build(even_ref, 0, wide)
     if spare:
-        build(rest_ref, pairs * wide, spare * TILE)
+        build(rest_ref, groups * wide, spare * TILE)
     coeffs = whole(0)
     coeffs_high, coeffs_low = split(coeffs)
     table = table_ref[...].reshape(snaps, 2 * LANES)
@@ -212,7 +214,7 @@
     left_ref[2 * order : 3 * order, :] = rates_low
     left_ref[3 * order : 4 * order, :] = along_low
     if spare:
-        multiply(rest_ref, pairs * wide, spare * TILE)
+        multiply(rest_ref, groups * wide, spare * TILE)
 
     def body(step, carry):
         first = 2 * step
@@ -222,10 +224,10 @@
         multiply(odd_ref, (first + 1) * wide, wide)
         return carry
 
-    lax.fori_loop(0, pairs // 2 - 1, body, 0)
-    build(odd_ref, (pairs - 1) * wide, wide)
-    multiply(even_ref, (pairs - 2) * wide, wide)
-    multiply(odd_ref, (pairs - 1) * wide, wide)
+    lax.fori_loop(0, groups // 2 - 1, body, 0)
+    build(odd_ref, (groups - 1) * wide, wide)
+    multiply(even_ref, (groups - 2) * wide, wide)
+    multiply(odd_ref, (groups - 1) * wide, wide)
 
     total = [jnp.sum(acc_ref[k], axis=1, keepdims=True) for k in range(4)]
     bb_extra, ss, ss_extra, bs_extra = total
@@ -340,9 +342,9 @@
             pltpu.VMEM((2, lanes, 2 * LANES), BF16),
             pltpu.VMEM((4 * order, snaps), BF16),
             pltpu.VMEM((2, snaps, snaps), BF16),
-            pltpu.VMEM((2, 2, lanes, 2 * TILE), BF16),
-            pltpu.VMEM((2, 2, lanes, 2 * TILE), BF16),
-            pltpu.VMEM((2, 2, lanes, max(padded // TILE % 4, 1) * TILE), BF16),
+            pltpu.VMEM((2, 2, lanes, GROUP * TILE), BF16),
+            pltpu.VMEM((2, 2, lanes, GROUP * TILE), BF16),
+            pltpu.VMEM((2, 2, lanes, max(padded // TILE % (2 * GROUP), 1) * TILE), BF16),
             pltpu.VMEM((order, padded), F32),
             pltpu.VMEM((order, padded), F32),
             pltpu.VMEM((order, snaps), F32),

time: 40.1 us -> 38.7 us (0.965)
  Pallas kernels: 12.9 us -> 11.5 us
    pallas_call x1, Pallas kernels: 9.72 us -> 8.33 us  [on_device(): pl.pallas_call(fit, out_shape=jax.ShapeDtypeStruct((order, width), F32),...]
  transfers between devices with their start and end apart: 2 -> 2, of which waited for: 1 -> 1; matrix products, arithmetic and copies ran while one was open for 2% -> 2% of each run, Pallas kernels for 3% -> 4%
where the time goes in v5:
time: 38.7 us; the launch traced here: 38.5 us
  blocking collectives  25.2 us (65%)
  Pallas kernels  11.5 us (30%)
  local copies, waits for them, and re-layouts  0.78 us (2%)
  starting transfers between devices  0.77 us (2%)
    all_to_all x1, blocking collectives, on_device(): pieces = lax.all_to_all(pieces, axes, 0, 0, tiled=True)  15.2 us
    all_to_all x1, blocking collectives, on_device(): half = lax.all_to_all(spread, axes, 0, 0, tiled=True)  9.97 us
    pallas_call x1, Pallas kernels, on_device(): pl.pallas_call(fit, out_shape=jax.ShapeDtypeStruct((order, width), F32),...  8.33 us
    pallas_call x1, Pallas kernels, on_device(): pl.pallas_call(project, in_specs=(smem,) + (pl.BlockSpec(memory_space=plt...  1.81 us
    pallas_call x1, Pallas kernels, on_device(): pl.pallas_call(lambda *refs: begin(order, width, *refs), in_specs=(vmem,)...  1.35 us
    reshape x1, local copies, waits for them, and re-layouts, on_device(): penalty.reshape(1, width)  0.78 us
  transfers between devices with their start and end apart: 2, of which 1 were waited for; matrix products, arithmetic and copies ran while one was open for 2% of the time, Pallas kernels for 4%

profile of v5, /device:TPU:0, one launch (start us, length us, event | category | flops | bytes accessed | tf_op | source)
XLA Modules:
  0.0 38.5 jit_solution(8534115480736453993)
XLA Ops:
  0.0 1.8 %project.1 = (f32[2,128,128]{2,1,0:T(8,128)S(1)}, f32[2,128,128]{2,1,0:T(8,128)S(1)}, s32[2,7260]{1,0:T(2,128)S(1)}) custom-call(s32[1]{0:T(128)} %bitcast.core_ref, bf16[120,1280]{1,0:T(8,128)(2,1)} %bitcast.8, bf16[1280,256]{1,0:T(8,128)(2,1)} %snaps_ref.1, bf16[1280,256]{1,0:T(8,128)(2,1)} %rates_ref.1, s32[2,7260]{1,0:T(2,128)} %pairs_ref.1), custom_call_target="tpu_custom_call" | custom-call | tf_op jit(solution)/shard_map/project/pallas_call | solution.py:290
  1.8 0.6 %collective-permute-start = (f32[2,128,128]{2,1,0:T(8,128)S(1)}, f32[2,128,128]{2,1,0:T(8,128)S(1)}, u32[]{:S(2)}, u32[]{:S(2)}) collective-permute-start(f32[2,128,128]{2,1,0:T(8,128)S(1)} %get-tuple-element.14), channel_id=1, source_target_pairs={{0,1},{1,0},{2,3},{3,2},{4,5},{5,4},{6,7},{7,6},{8,9},{9,8},{10,11... | collective-permute-start | bytes 393224 | tf_op jit(solution)/shard_map/ppermute | solution.py:305
  2.4 0.8 %reshape.12.weight_ref = f32[1,7381]{1,0:T(1,128)S(1)} reshape(f32[7381]{0:T(1024)} %param.9) | data formatting | bytes 59048 | tf_op jit(solution)/shard_map/reshape | solution.py:305
  3.2 0.2 collective-permute-done
  3.4 15.2 %all_to_all.10.parts_ref = f32[32,8,128]{2,1,0:T(8,128)S(1)} all-to-all(f32[32,8,128]{2,1,0:T(8,128)S(1)} %bitcast.7), channel_id=1, replica_groups=mesh['gx'=8,'gy'=4] {'gx','gy'}, dimensions={0} | all-to-all | bytes 262144 | tf_op jit(solution)/shard_map/all_to_all | solution.py:310
  18.6 10.0 %all_to_all.11 = f32[32,8,128]{2,1,0:T(8,128)S(1)} all-to-all(f32[32,8,128]{2,1,0:T(8,128)S(1)} %add_up.1), channel_id=1, replica_groups=mesh['gx'=8,'gy'=4] {'gx','gy'}, dimensions={0} | all-to-all | bytes 262144 | tf_op jit(solution)/shard_map/all_to_all | solution.py:318
  28.6 0.2 collective-permute-start.1
  28.8 1.4 %begin.1 = (bf16[2,128,7424]{2,1,0:T(8,128)(2,1)S(1)}, bf16[2,128,7424]{2,1,0:T(8,128)(2,1)S(1)}, bf16[128,256]{1,0:T(8,128)(2,1)S(1)}) custom-call(f32[2,128,128]{2,1,0:T(8,128)S(1)} %bitcast.5, s32[2,7260]{1,0:T(2,128)S(1)} %get-tuple-element.16.refs_1_), custom_call_target="tpu_custom_call" | custom-call | flops 2000000000 | bytes 8000000 | tf_op jit(solution)/shard_map/begin/pallas_call | solution.py:321
  30.2 0.0 collective-permute-done.1.other_ref
  30.2 8.3 %fit.1 = f32[120,7381]{1,0:T(8,128)} custom-call(s32[1]{0:T(128)} %bitcast.core_ref, f32[2,128,128]{2,1,0:T(8,128)S(1)} %bitcast.6, f32[2,128,128]{2,1,0:T(8,128)S(1)} %collective-permute-done.1.other_ref, bf16[2,128,7424]{2,1,0:T(8,128)(2,1)S(1)} %get-tuple-element.17.ready_ref, bf16[2,128,7424]{2,1,0:T(8,128)(2,1)S(1)} %get-tuple-element.18.hot_ref, ...), custom_call_target="tpu_custom_call" | custom-call | tf_op jit(solution)/shard_map/fit/pallas_call | solution.py:335
  (2 shorter events, 0.0 us)
Async XLA Ops:
  1.8 1.5 %collective-permute-start = (f32[2,128,128]{2,1,0:T(8,128)S(1)}, f32[2,128,128]{2,1,0:T(8,128)S(1)}, u32[]{:S(2)}, u32[]{:S(2)}) collective-permute-start(f32[2,128,128]{2,1,0:T(8,128)S(1)} %get-tuple-element.14), channel_id=1, source_target_pairs={{0,1},{1,0},{2,3},{3,2},{4,5},{5,4},{6,7},{7,6},{8,9},{9,8},{10,11... | collective-permute-start | bytes 393224 | tf_op jit(solution)/shard_map/ppermute | solution.py:305
  28.6 1.6 %collective-permute-start.1 = (f32[2,128,128]{2,1,0:T(8,128)S(1)}, f32[2,128,128]{2,1,0:T(8,128)S(1)}, u32[]{:S(2)}, u32[]{:S(2)}) collective-permute-start(f32[2,128,128]{2,1,0:T(8,128)S(1)} %bitcast.4), channel_id=1, source_target_pairs={{0,1},{1,0},{2,3},{3,2},{4,5},{5,4},{6,7},{7,6},{8,9},{9,8},{10,11... | collective-permute-start | bytes 393224 | tf_op jit(solution)/shard_map/ppermute | solution.py:320
